TPU v7x, 512 devices: a whole 4x8x8 slice. The times are simulated.
512 devices in a mesh: sp: 4 (over x), bn: 8 (over z), dp: 16 (over y, core).
Axes of the slice: x: 4, y: 8, z: 8, core: 2. Of those that a mesh axis runs over, the one named last changes fastest.
Arguments:
- images: bfloat16 [128, 4, 64, 40, 128], P(('bn', 'dp'), 'sp'), may hold values from -8 to 8, as said below
- out_grad: bfloat16 [128, 4, 256, 40, 128], P(('bn', 'dp'), 'sp'), may hold values from -8 to 8, as said below
- conv_weight: bfloat16 [3, 3, 64, 64], replicated, may hold values from -0.25 to 0.25
- proj_weight: bfloat16 [64, 256], replicated, may hold values from -0.75 to 0.75
- gain_one: float32 [64], replicated, may hold values from 0.1 to 1.9
- shift_one: float32 [64], replicated, may hold values from -3 to 3
- gain_three: float32 [256], replicated, may hold values from 0.1 to 1.9
- shift_three: float32 [256], replicated, may hold values from -3 to 3
Outputs:
- images_grad: bfloat16 [128, 4, 64, 40, 128], P(('bn', 'dp'), 'sp')
- conv_grad: float32 [3, 3, 64, 64], replicated
- proj_grad: float32 [64, 256], replicated
- gain_one_grad: float32 [64], replicated
- shift_one_grad: float32 [64], replicated
- gain_three_grad: float32 [256], replicated
- shift_three_grad: float32 [256], replicated
Inputs may be any that keep to these rules, and one draw needn't show every extreme that they name: `images`: channels of one quadrant have their own offset and spread. `out_grad`: channels of one quadrant have their own offset and spread.
All inputs are finite; a program needn't handle non-finite values.
Results may differ from a plain program's by a relative error of at most 0.029.
Values may be sent and summed in bfloat16 or wider, within the bound.
A program may use at most 64 MiB of HBM per device.

v0:
```python
import jax
import jax.numpy as jnp
from jax import lax
from jax.sharding import PartitionSpec as P

norm_floor = 1e-05


def from_partner(value, axis, distance):
    return lax.ppermute(value, axis, [(i, i ^ 1 << distance) for i in range(lax.axis_size(axis))])


def sent_to_all(value, axis):
    copies = jnp.broadcast_to(value, (lax.axis_size(axis), *value.shape))
    return lax.all_to_all(copies, axis, split_axis=0, concat_axis=0, tiled=True)


def of_everyone(value, axis):
    everything = sent_to_all(value, axis)
    return jnp.sum(everything, axis=0)


def together(arrays, axis):
    line, at, finished = (jnp.concatenate([a.reshape(-1) for a in arrays]), 0, [])
    so_far = of_everyone(line, axis)
    for a in arrays:
        finished.append(so_far[at : at + a.size].reshape(a.shape))
        at += a.size
    return tuple(finished)


def cut_along(value, dim, length):
    shape = value.shape
    tiles = value.reshape(*shape[:dim], length, shape[dim] // length, *shape[dim + 1 :])
    return jnp.moveaxis(tiles, dim, 0)


def sum_at_owner(value, axis, dim):
    length = lax.axis_size(axis)
    tiles = lax.all_to_all(cut_along(value, dim, length), axis, 0, 0, tiled=True)
    return jnp.sum(tiles.astype(jnp.float32), axis=0)


def joined_along(tiles, dim):
    shape = list(tiles.shape[1:])
    shape[dim] *= tiles.shape[0]
    return jnp.moveaxis(tiles, 0, dim).reshape(shape)


def gather_together(arrays, axis, dims):
    line = jnp.concatenate([a.reshape(-1) for a in arrays])
    lines, at, finished = (lax.all_gather(line, axis), 0, [])
    for a, dim in zip(arrays, dims):
        tiles = lines[:, at : at + a.size].reshape(-1, *a.shape)
        finished.append(joined_along(tiles, dim))
        at += a.size
    return tuple(finished)


def silu_slope(inputs):
    sigma = jax.nn.sigmoid(inputs)
    return sigma * (1.0 + inputs * (1.0 - sigma))


def channel(vector):
    return vector[None, :, None, None]


def extend(field):
    position = lax.axis_index("sp")
    column = position % 2
    row_half = position // 2
    edge_cols = jnp.where(column == 0, field[:, :, :, -1:], field[:, :, :, :1])
    across = from_partner(edge_cols, "sp", 0)
    empty_cols = jnp.zeros_like(across)
    left_side = jnp.where(column == 1, across, empty_cols)
    right_side = jnp.where(column == 0, across, empty_cols)
    wider = jnp.concatenate([left_side, field, right_side], axis=3)
    edge_rows = jnp.where(row_half == 0, wider[:, :, -1:, :], wider[:, :, :1, :])
    incoming = from_partner(edge_rows, "sp", 1)
    empty_rows = jnp.zeros_like(incoming)
    top_side = jnp.where(row_half == 1, incoming, empty_rows)
    bottom_side = jnp.where(row_half == 0, incoming, empty_rows)
    return jnp.concatenate([top_side, wider, bottom_side], axis=2)


def conv_cells(padded, kernel, tile_rows, tile_cols):
    summed = None
    for row_off in range(3):
        for col_off in range(3):
            window = padded[:, :, row_off : row_off + tile_rows, col_off : col_off + tile_cols]
            partial_sum = jnp.einsum(
                "oi,nihw->nohw",
                kernel[row_off, col_off],
                window,
                preferred_element_type=jnp.float32,
            )
            summed = partial_sum if summed is None else summed + partial_sum
    return summed


def conv_back(padded, kernel, tile_rows, tile_cols):
    summed = None
    for row_off in range(3):
        for col_off in range(3):
            window = padded[
                :, :, 2 - row_off : 2 - row_off + tile_rows, 2 - col_off : 2 - col_off + tile_cols
            ]
            partial_sum = jnp.einsum(
                "oi,nohw->nihw",
                kernel[row_off, col_off],
                window,
                preferred_element_type=jnp.float32,
            )
            summed = partial_sum if summed is None else summed + partial_sum
    return summed


def kernel_grad(padded, grad_conv_out, tile_rows, tile_cols):
    pieces_list = []
    for row_off in range(3):
        for col_off in range(3):
            window = padded[:, :, row_off : row_off + tile_rows, col_off : col_off + tile_cols]
            pieces_list.append(
                jnp.einsum(
                    "nohw,nihw->oi", grad_conv_out, window, preferred_element_type=jnp.float32
                )
            )
    depth = grad_conv_out.shape[1]
    return jnp.stack(pieces_list).reshape(3, 3, depth, depth)


def group_moments(values, cell_count):
    totals = of_everyone(jnp.sum(values, axis=(0, 2, 3)), ("sp", "bn"))
    average = totals / cell_count
    centred = values - channel(average)
    squares = of_everyone(jnp.sum(centred * centred, axis=(0, 2, 3)), ("sp", "bn"))
    return (average, squares / cell_count)


def norm_backward(grad_pre, normed, gain, scale, cell_count):
    local_sum = jnp.sum(grad_pre, axis=(0, 2, 3))
    local_cross = jnp.sum(grad_pre * normed, axis=(0, 2, 3))
    group_sum, group_cross = together((local_sum, local_cross), ("sp", "bn"))
    grad_in = channel(gain * scale) * (
        grad_pre - channel(group_sum) / cell_count - normed * channel(group_cross) / cell_count
    )
    return (grad_in.astype(jnp.bfloat16), local_sum, local_cross, group_sum, group_cross)


def shards(
    images, out_grad, conv_weight, proj_weight, gain_one, shift_one, gain_three, shift_three
):
    field = images[:, 0]
    cotangent = out_grad[:, 0]
    batch, depth, tile_rows, tile_cols = field.shape
    quadrants = lax.axis_size("sp")
    cell_count = float(quadrants * lax.axis_size("bn") * batch * tile_rows * tile_cols)
    per_image = 1.0 / float(quadrants * tile_rows * tile_cols)
    padded = extend(field)
    conv_out = conv_cells(padded, conv_weight, tile_rows, tile_cols)
    mean_one, var_one = group_moments(conv_out, cell_count)
    scale_one = lax.rsqrt(var_one + norm_floor)
    normed_one = (conv_out - channel(mean_one)) * channel(scale_one)
    before_act = channel(gain_one) * normed_one + channel(shift_one)
    hidden = jax.nn.silu(before_act).astype(jnp.bfloat16)
    widened = jnp.einsum("io,nihw->nohw", proj_weight, hidden, preferred_element_type=jnp.float32)
    mean_three, var_three = group_moments(widened, cell_count)
    scale_three = lax.rsqrt(var_three + norm_floor)
    normed_three = (widened - channel(mean_three)) * channel(scale_three)
    output_pre = channel(gain_three) * normed_three + channel(shift_three)
    grad_out = cotangent.astype(jnp.float32) * silu_slope(output_pre)
    grad_wide, sum_three, cross_three, group_sum_three, group_cross_three = norm_backward(
        grad_out, normed_three, gain_three, scale_three, cell_count
    )
    grad_proj = jnp.einsum("nihw,nohw->io", hidden, grad_wide, preferred_element_type=jnp.float32)
    grad_hidden = jnp.einsum(
        "io,nohw->nihw", proj_weight, grad_wide, preferred_element_type=jnp.float32
    )
    grad_pre = grad_hidden * silu_slope(before_act)
    grad_conv_out, sum_one, cross_one, group_sum_one, group_cross_one = norm_backward(
        grad_pre, normed_one, gain_one, scale_one, cell_count
    )
    grad_kernel = kernel_grad(padded, grad_conv_out, tile_rows, tile_cols)
    back_pad = extend(grad_conv_out)
    grad_field = conv_back(back_pad, conv_weight, tile_rows, tile_cols).astype(jnp.bfloat16)
    kernel_rows = grad_kernel.reshape(9 * depth, depth)
    part_kernel, part_proj = (
        sum_at_owner(kernel_rows.astype(jnp.bfloat16), ("sp", "bn"), 0),
        sum_at_owner(grad_proj.astype(jnp.bfloat16), ("sp", "bn"), 0),
    )
    part_kernel, part_proj, cross_one, sum_one, cross_three, sum_three = together(
        (
            part_kernel,
            part_proj,
            group_cross_one,
            group_sum_one,
            group_cross_three,
            group_sum_three,
        ),
        "dp",
    )
    full_kernel, full_proj = gather_together((part_kernel, part_proj), ("sp", "bn"), (0, 0))
    kernel_total = full_kernel.reshape(3, 3, depth, depth)
    return (
        grad_field[:, None],
        kernel_total * per_image,
        full_proj * per_image,
        cross_one * per_image,
        sum_one * per_image,
        cross_three * per_image,
        sum_three * per_image,
    )


def solution(mesh):
    in_specs = (
        P(("bn", "dp"), "sp", None, None, None),
        P(("bn", "dp"), "sp", None, None, None),
        P(),
        P(),
        P(),
        P(),
        P(),
        P(),
    )
    out_specs = (P(("bn", "dp"), "sp", None, None, None), P(), P(), P(), P(), P(), P())
    return jax.shard_map(shards, mesh=mesh, in_specs=in_specs, out_specs=out_specs, check_vma=False)
```

profile of v0, /device:TPU:6, one launch (start us, length us, event | category | flops | bytes accessed | tf_op | source)
XLA Modules:
  0.0 257.9 jit_solution(12140756275401114393)
XLA Ops:
  2.5 2.7 %collective-permute-start = (bf16[1,64,40,1]{1,2,3,0:T(8,128)(2,1)S(1)}, bf16[1,64,40,1]{1,2,3,0:T(8,128)(2,1)S(1)}, u32[]{:S(2)}, u32[]{:S(2)}) collective-permute-start(bf16[1,64,40,1]{1,2,3,0:T(8,128)(2,1)S(1)} %copy.92), channel_id=1, source_target_pairs={{0,128},{128,0},{256,384},{384,256},{1,129},{129,1},{257,385},{385... | collective-permute-start | bytes 15368 | tf_op jit(solution)/shard_map/ppermute | solution.py:10
  5.2 2.8 %collective-permute-done = bf16[1,64,40,1]{1,2,3,0:T(8,128)(2,1)S(1)} collective-permute-done((bf16[1,64,40,1]{1,2,3,0:T(8,128)(2,1)S(1)}, bf16[1,64,40,1]{1,2,3,0:T(8,128)(2,1)S(1)}, u32[]{:S(2)}, u32[]{:S(2)}) %collective-permute-start) | collective-permute-done | bytes 5152 | tf_op jit(solution)/shard_map/ppermute | solution.py:10
  8.7 7.2 %collective-permute-start.1 = (bf16[1,64,1,130]{3,1,2,0:T(8,128)(2,1)S(1)}, bf16[1,64,1,130]{3,1,2,0:T(8,128)(2,1)S(1)}, u32[]{:S(2)}, u32[]{:S(2)}) collective-permute-start(bf16[1,64,1,130]{3,1,2,0:T(8,128)(2,1)S(1)} %fusion.76), channel_id=1, source_target_pairs={{0,256},{128,384},{256,0},{384,128},{1,257},{129,385},{257,1},{385... | collective-permute-start | bytes 49928 | tf_op jit(solution)/shard_map/ppermute | solution.py:10
  15.9 1.9 collective-permute-done.1
  17.8 1.8 pad_maximum_fusion
  24.5 19.6 %all_to_all.52 = f32[32,1,64]{2,1,0:T(1,128)S(1)} all-to-all(f32[32,1,64]{2,1,0:T(1,128)S(1)} %broadcast_in_dim.16), channel_id=1, replica_groups=mesh['sp'=4,'bn'=8,'dp'=16] {'sp','bn'}, dimensions={0} | all-to-all | bytes 16384 | tf_op jit(solution)/shard_map/all_to_all | solution.py:15
  44.4 12.7 %all_to_all.53 = f32[32,1,64]{2,1,0:T(1,128)S(1)} all-to-all(f32[32,1,64]{2,1,0:T(1,128)S(1)} %broadcast_in_dim.17), channel_id=1, replica_groups=mesh['sp'=4,'bn'=8,'dp'=16] {'sp','bn'}, dimensions={0} | all-to-all | bytes 16384 | tf_op jit(solution)/shard_map/all_to_all | solution.py:15
  57.7 3.8 %fusion.128 = (f32[256]{0:T(256)S(1)}, f32[40,128,256]{2,1,0:T(8,128)}) fusion(bf16[64,256]{1,0:T(8,128)(2,1)S(1)} %copy-done, f32[64]{0:T(128)S(1)} %copy-done.34, f32[64]{0:T(128)S(1)} %get-tuple-element.71, f32[64]{0:T(128)S(1)} %broadcast_multiply_fusion.3, f32[40,128,64]{1,2,0:T(8,128)S(1)} %get-tuple-element.73, f32[64]{0:T(128)S(1)} %copy-done.32), kind=kOutput, calls=%fused_computation.214 | convolution fusion | flops 172031744 | bytes 6588416 | tf_op jit(solution)/shard_map/io,nihw->nohw/dot_general | solution.py:167
  61.6 12.8 %all_to_all.54 = f32[32,1,256]{2,1,0:T(1,128)S(1)} all-to-all(f32[32,1,256]{2,1,0:T(1,128)S(1)} %broadcast_in_dim.18), channel_id=1, replica_groups=mesh['sp'=4,'bn'=8,'dp'=16] {'sp','bn'}, dimensions={0} | all-to-all | bytes 65536 | tf_op jit(solution)/shard_map/all_to_all | solution.py:15
  74.5 3.2 %multiply_reduce_fusion = f32[256]{0:T(256)S(1)} fusion(f32[40,128,256]{2,1,0:T(8,128)} %get-tuple-element.75, f32[256]{0:T(256)S(1)} %broadcast_multiply_fusion.1), kind=kLoop, calls=%fused_computation.11 | loop fusion | flops 3931904 | bytes 5244928 | tf_op jit(solution)/shard_map/reduce_sum | solution.py:137
  78.3 5.8 %all-to-all-start.3 = ((f32[32,1,256]{2,1,0:T(1,128)}), f32[32,1,256]{2,1,0:T(1,128)S(1)}, u32[]{:S(2)}, u32[]{:S(2)}) async-start(f32[32,1,256]{2,1,0:T(1,128)} %broadcast_in_dim.19), calls=%async_computation.3 | async-start | bytes 65536 | tf_op jit(solution)/shard_map/all_to_all | solution.py:15
  84.1 3.9 %copy.100 = bf16[1,1,256,40,128]{2,4,3,1,0:T(8,128)(2,1)S(1)} copy(bf16[1,1,256,40,128]{4,3,2,1,0:T(8,128)(2,1)} %param.9) | data formatting | bytes 5242880 | tf_op args[1]
  88.1 3.9 %all-to-all-done.3 = f32[32,1,256]{2,1,0:T(1,128)S(1)} async-done(((f32[32,1,256]{2,1,0:T(1,128)}), f32[32,1,256]{2,1,0:T(1,128)S(1)}, u32[]{:S(2)}, u32[]{:S(2)}) %all-to-all-start.3) | async-done | bytes 32800 | tf_op jit(solution)/shard_map/all_to_all | solution.py:15
  92.1 4.7 %fusion.123 = (f32[256]{0:T(256)S(1)}, f32[256]{0:T(256)S(1)}) fusion(f32[256]{0:T(256)S(1)} %copy-done.23, f32[256]{0:T(256)S(1)} %get-tuple-element.66, f32[256]{0:T(256)S(1)} %broadcast_multiply_fusion.1, f32[40,128,256]{2,1,0:T(8,128)} %get-tuple-element.75, f32[256]{0:T(256)S(1)} %copy-done.17, bf16[1,1,256,40,128]{2,4,3,1,0:T(8,128)(2,1)S(1)} %copy.100), kind=kLoop, calls=%fused_computation.209 | loop fusion | flops 20971008 | bytes 7870464 | tf_op jit(solution)/shard_map/reduce_sum | solution.py:142
  96.9 13.8 %all_to_all.55 = f32[32,1,512]{2,1,0:T(1,128)S(1)} all-to-all(f32[32,1,512]{2,1,0:T(1,128)S(1)} %broadcast_in_dim.20), channel_id=1, replica_groups=mesh['sp'=4,'bn'=8,'dp'=16] {'sp','bn'}, dimensions={0} | all-to-all | bytes 131072 | tf_op jit(solution)/shard_map/all_to_all | solution.py:15
  111.3 5.3 %fusion.7 = bf16[256,40,128]{0,2,1:T(8,128)(2,1)S(1)} fusion(f32[40,128,256]{2,1,0:T(8,128)} %get-tuple-element.75, f32[256]{0:T(256)S(1)} %get-tuple-element.64, f32[256]{0:T(256)S(1)} %get-tuple-element.63, f32[256]{0:T(256)S(1)} %get-tuple-element.66, f32[256]{0:T(256)S(1)} %get-tuple-element.65, f32[256]{0:T(256)} %copy-done.16, f32[256]{0:T(256)S(1)} %copy-done.24, ...), kind=kLoop, calls=%fused_computation.13 | loop fusion | flops 24903680 | bytes 10492928 | tf_op jit(solution)/shard_map/reshape.43
  116.7 2.2 fusion.124
  119.6 5.7 %all-to-all-start.5 = ((f32[32,1,128]{2,1,0:T(1,128)}), f32[32,1,128]{2,1,0:T(1,128)S(1)}, u32[]{:S(2)}, u32[]{:S(2)}) async-start(f32[32,1,128]{2,1,0:T(1,128)} %broadcast_in_dim.21), calls=%async_computation.5 | async-start | bytes 32768 | tf_op jit(solution)/shard_map/all_to_all | solution.py:15
  125.3 2.4 fusion.18
  128.3 4.8 %all-to-all-done.5 = f32[32,1,128]{2,1,0:T(1,128)S(1)} async-done(((f32[32,1,128]{2,1,0:T(1,128)}), f32[32,1,128]{2,1,0:T(1,128)S(1)}, u32[]{:S(2)}, u32[]{:S(2)}) %all-to-all-start.5) | async-done | bytes 16416 | tf_op jit(solution)/shard_map/all_to_all | solution.py:15
  133.1 5.8 %all-to-all-start.7 = ((bf16[32,2,256]{2,1,0:T(2,128)(2,1)}), bf16[32,2,256]{2,1,0:T(2,128)(2,1)S(1)}, u32[]{:S(2)}, u32[]{:S(2)}) async-start(bf16[32,2,256]{2,1,0:T(2,128)(2,1)} %reshape.257), calls=%async_computation.7 | async-start | bytes 65536 | tf_op jit(solution)/shard_map/all_to_all | solution.py:40
  139.5 1.8 fusion.15
  149.2 2.7 %collective-permute-start.2 = (bf16[1,64,40,1]{1,2,3,0:T(8,128)(2,1)S(1)}, bf16[1,64,40,1]{1,2,3,0:T(8,128)(2,1)S(1)}, u32[]{:S(2)}, u32[]{:S(2)}) collective-permute-start(bf16[1,64,40,1]{1,2,3,0:T(8,128)(2,1)S(1)} %copy.104), channel_id=1, source_target_pairs={{0,128},{128,0},{256,384},{384,256},{1,129},{129,1},{257,385},{385... | collective-permute-start | bytes 15368 | tf_op jit(solution)/shard_map/ppermute | solution.py:10
  153.0 1.8 collective-permute-done.2
  157.2 3.5 %collective-permute-start.3 = (bf16[1,64,1,130]{3,1,2,0:T(8,128)(2,1)S(1)}, bf16[1,64,1,130]{3,1,2,0:T(8,128)(2,1)}, u32[]{:S(2)}, u32[]{:S(2)}) collective-permute-start(bf16[1,64,1,130]{3,1,2,0:T(8,128)(2,1)S(1)} %fusion.75), channel_id=1, source_target_pairs={{0,256},{128,384},{256,0},{384,128},{1,257},{129,385},{257,1},{385... | collective-permute-start | bytes 49928 | tf_op jit(solution)/shard_map/ppermute | solution.py:10
  165.4 1.8 maximum_maximum_fusion.1
  171.0 9.8 %all-to-all-start.6 = ((bf16[32,2,576]{2,1,0:T(2,128)(2,1)}), bf16[32,2,576]{2,1,0:T(2,128)(2,1)S(1)}, u32[]{:S(2)}, u32[]{:S(2)}) async-start(bf16[32,2,576]{2,1,0:T(2,128)(2,1)} %reshape.304), calls=%async_computation.6 | async-start | bytes 163840 | tf_op jit(solution)/shard_map/all_to_all | solution.py:40
  180.9 1.7 convolution_add_fusion.10
  182.7 6.4 %all-to-all-done.6 = bf16[32,2,576]{2,1,0:T(2,128)(2,1)S(1)} async-done(((bf16[32,2,576]{2,1,0:T(2,128)(2,1)}), bf16[32,2,576]{2,1,0:T(2,128)(2,1)S(1)}, u32[]{:S(2)}, u32[]{:S(2)}) %all-to-all-start.6) | async-done | bytes 73760 | tf_op jit(solution)/shard_map/all_to_all | solution.py:40
  190.1 7.2 %all-to-all-start.8 = ((f32[16,1,2304]{2,1,0:T(1,128)}), f32[16,1,2304]{2,1,0:T(1,128)}, u32[]{:S(2)}, u32[]{:S(2)}) async-start(f32[16,1,2304]{2,1,0:T(1,128)} %broadcast_in_dim.23), calls=%async_computation.8 | async-start | bytes 294912 | tf_op jit(solution)/shard_map/all_to_all | solution.py:15
  199.5 6.9 %all-to-all-done.8 = f32[16,1,2304]{2,1,0:T(1,128)} async-done(((f32[16,1,2304]{2,1,0:T(1,128)}), f32[16,1,2304]{2,1,0:T(1,128)}, u32[]{:S(2)}, u32[]{:S(2)}) %all-to-all-start.8) | async-done | bytes 147488 | tf_op jit(solution)/shard_map/all_to_all | solution.py:15
  208.6 47.8 %all-gather.1 = f32[32,1,1664]{2,1,0:T(1,128)S(1)} all-gather(f32[1,1,1664]{2,1,0:T(1,128)S(1)} %reshape.272), channel_id=2, replica_groups=mesh['sp'=4,'bn'=8,'dp'=16] {'sp','bn'}, dimensions={0}, use_global_device_ids=true | all-gather | bytes 219648 | tf_op jit(solution)/shard_map/all_gather | solution.py:52
  (155 shorter events, 38.2 us)
Async XLA Ops:
  0.6 57.1 %copy-start = (bf16[64,256]{1,0:T(8,128)(2,1)S(1)}, bf16[64,256]{1,0:T(8,128)(2,1)}, u32[]{:S(2)}) copy-start(bf16[64,256]{1,0:T(8,128)(2,1)} %param.11) | copy-start | bytes 98308
  2.5 5.6 %collective-permute-start = (bf16[1,64,40,1]{1,2,3,0:T(8,128)(2,1)S(1)}, bf16[1,64,40,1]{1,2,3,0:T(8,128)(2,1)S(1)}, u32[]{:S(2)}, u32[]{:S(2)}) collective-permute-start(bf16[1,64,40,1]{1,2,3,0:T(8,128)(2,1)S(1)} %copy.92), channel_id=1, source_target_pairs={{0,128},{128,0},{256,384},{384,256},{1,129},{129,1},{257,385},{385... | collective-permute-start | bytes 15368 | tf_op jit(solution)/shard_map/ppermute | solution.py:10
  8.6 12.6 %copy-start.3 = (bf16[1,64,40,1]{3,1,2,0:T(8,128)(2,1)}, bf16[1,64,40,1]{3,1,2,0:T(8,128)(2,1)S(1)}, u32[]{:S(2)}) copy-start(bf16[1,64,40,1]{3,1,2,0:T(8,128)(2,1)S(1)} %get-tuple-element.52) | copy-start | bytes 15364
  8.6 14.0 %copy-start.1 = (bf16[1,64,40,1]{3,1,2,0:T(8,128)(2,1)}, bf16[1,64,40,1]{3,1,2,0:T(8,128)(2,1)S(1)}, u32[]{:S(2)}) copy-start(bf16[1,64,40,1]{3,1,2,0:T(8,128)(2,1)S(1)} %get-tuple-element.53) | copy-start | bytes 15364
  8.7 9.1 %collective-permute-start.1 = (bf16[1,64,1,130]{3,1,2,0:T(8,128)(2,1)S(1)}, bf16[1,64,1,130]{3,1,2,0:T(8,128)(2,1)S(1)}, u32[]{:S(2)}, u32[]{:S(2)}) collective-permute-start(bf16[1,64,1,130]{3,1,2,0:T(8,128)(2,1)S(1)} %fusion.76), channel_id=1, source_target_pairs={{0,256},{128,384},{256,0},{384,128},{1,257},{129,385},{257,1},{385... | collective-permute-start | bytes 49928 | tf_op jit(solution)/shard_map/ppermute | solution.py:10
  24.4 37.1 %copy-start.5 = (f32[40,128,64]{1,2,0:T(8,128)}, f32[40,128,64]{1,2,0:T(8,128)S(1)}, u32[]{:S(2)}) copy-start(f32[40,128,64]{1,2,0:T(8,128)S(1)} %get-tuple-element.73) | copy-start | bytes 3932164
  24.4 32.7 %copy-start.32 = (f32[64]{0:T(128)S(1)}, f32[64]{0:T(128)}, u32[]{:S(2)}) copy-start(f32[64]{0:T(128)} %param.12) | copy-start | bytes 772
  24.5 33.3 %copy-start.34 = (f32[64]{0:T(128)S(1)}, f32[64]{0:T(128)}, u32[]{:S(2)}) copy-start(f32[64]{0:T(128)} %param.13) | copy-start | bytes 772
  44.1 17.5 %copy-start.26 = (f32[64]{0:T(128)}, f32[64]{0:T(128)S(1)}, u32[]{:S(2)}) copy-start(f32[64]{0:T(128)S(1)} %broadcast_multiply_fusion.3) | copy-start | bytes 772
  74.5 17.6 %copy-start.16 = (f32[256]{0:T(256)}, f32[256]{0:T(256)S(1)}, u32[]{:S(2)}) copy-start(f32[256]{0:T(256)S(1)} %broadcast_multiply_fusion.1) | copy-start | bytes 3076
  78.3 13.7 %all-to-all-start.3 = ((f32[32,1,256]{2,1,0:T(1,128)}), f32[32,1,256]{2,1,0:T(1,128)S(1)}, u32[]{:S(2)}, u32[]{:S(2)}) async-start(f32[32,1,256]{2,1,0:T(1,128)} %broadcast_in_dim.19), calls=%async_computation.3 | async-start | bytes 65536 | tf_op jit(solution)/shard_map/all_to_all | solution.py:15
  84.1 8.0 %copy-start.17 = (f32[256]{0:T(256)S(1)}, f32[256]{0:T(256)}, u32[]{:S(2)}) copy-start(f32[256]{0:T(256)} %param.14) | copy-start | bytes 3076
  84.1 8.0 %copy-start.23 = (f32[256]{0:T(256)S(1)}, f32[256]{0:T(256)}, u32[]{:S(2)}) copy-start(f32[256]{0:T(256)} %param.15) | copy-start | bytes 3076
  92.1 19.2 %copy-start.18 = (f32[256]{0:T(256)S(1)}, f32[256]{0:T(256)}, u32[]{:S(2)}) copy-start(f32[256]{0:T(256)} %param.14) | copy-start | bytes 3076
  92.1 19.2 %copy-start.24 = (f32[256]{0:T(256)S(1)}, f32[256]{0:T(256)}, u32[]{:S(2)}) copy-start(f32[256]{0:T(256)} %param.15) | copy-start | bytes 3076
  111.3 5.4 %copy-start.6 = (f32[40,128,64]{1,2,0:T(8,128)S(1)}, f32[40,128,64]{1,2,0:T(8,128)}, u32[]{:S(2)}) copy-start(f32[40,128,64]{1,2,0:T(8,128)} %copy-done.5) | copy-start | bytes 3932164
  111.3 5.4 %copy-start.27 = (f32[64]{0:T(128)S(1)}, f32[64]{0:T(128)}, u32[]{:S(2)}) copy-start(f32[64]{0:T(128)} %copy-done.26) | copy-start | bytes 772
  111.3 5.4 %copy-start.30 = (f32[64]{0:T(128)S(1)}, f32[64]{0:T(128)}, u32[]{:S(2)}) copy-start(f32[64]{0:T(128)} %copy-done.29) | copy-start | bytes 772
  111.3 5.4 %copy-start.33 = (f32[64]{0:T(128)S(1)}, f32[64]{0:T(128)}, u32[]{:S(2)}) copy-start(f32[64]{0:T(128)} %param.12) | copy-start | bytes 772
  111.3 5.4 %copy-start.35 = (f32[64]{0:T(128)S(1)}, f32[64]{0:T(128)}, u32[]{:S(2)}) copy-start(f32[64]{0:T(128)} %param.13) | copy-start | bytes 772
  116.7 8.6 %copy-start.7 = (f32[40,128,64]{1,2,0:T(8,128)S(1)}, f32[40,128,64]{1,2,0:T(8,128)}, u32[]{:S(2)}) copy-start(f32[40,128,64]{1,2,0:T(8,128)} %copy-done.5) | copy-start | bytes 3932164
  119.6 13.5 %all-to-all-start.5 = ((f32[32,1,128]{2,1,0:T(1,128)}), f32[32,1,128]{2,1,0:T(1,128)S(1)}, u32[]{:S(2)}, u32[]{:S(2)}) async-start(f32[32,1,128]{2,1,0:T(1,128)} %broadcast_in_dim.21), calls=%async_computation.5 | async-start | bytes 32768 | tf_op jit(solution)/shard_map/all_to_all | solution.py:15
  125.3 14.1 %copy-start.28 = (f32[64]{0:T(128)S(1)}, f32[64]{0:T(128)}, u32[]{:S(2)}) copy-start(f32[64]{0:T(128)} %get-tuple-element.70) | copy-start | bytes 772
  133.1 37.9 %all-to-all-start.7 = ((bf16[32,2,256]{2,1,0:T(2,128)(2,1)}), bf16[32,2,256]{2,1,0:T(2,128)(2,1)S(1)}, u32[]{:S(2)}, u32[]{:S(2)}) async-start(bf16[32,2,256]{2,1,0:T(2,128)(2,1)} %reshape.257), calls=%async_computation.7 | async-start | bytes 65536 | tf_op jit(solution)/shard_map/all_to_all | solution.py:40
  149.2 5.6 %collective-permute-start.2 = (bf16[1,64,40,1]{1,2,3,0:T(8,128)(2,1)S(1)}, bf16[1,64,40,1]{1,2,3,0:T(8,128)(2,1)S(1)}, u32[]{:S(2)}, u32[]{:S(2)}) collective-permute-start(bf16[1,64,40,1]{1,2,3,0:T(8,128)(2,1)S(1)} %copy.104), channel_id=1, source_target_pairs={{0,128},{128,0},{256,384},{384,256},{1,129},{129,1},{257,385},{385... | collective-permute-start | bytes 15368 | tf_op jit(solution)/shard_map/ppermute | solution.py:10
  157.2 7.4 %collective-permute-start.3 = (bf16[1,64,1,130]{3,1,2,0:T(8,128)(2,1)S(1)}, bf16[1,64,1,130]{3,1,2,0:T(8,128)(2,1)}, u32[]{:S(2)}, u32[]{:S(2)}) collective-permute-start(bf16[1,64,1,130]{3,1,2,0:T(8,128)(2,1)S(1)} %fusion.75), channel_id=1, source_target_pairs={{0,256},{128,384},{256,0},{384,128},{1,257},{129,385},{257,1},{385... | collective-permute-start | bytes 49928 | tf_op jit(solution)/shard_map/ppermute | solution.py:10
  171.0 18.0 %all-to-all-start.6 = ((bf16[32,2,576]{2,1,0:T(2,128)(2,1)}), bf16[32,2,576]{2,1,0:T(2,128)(2,1)S(1)}, u32[]{:S(2)}, u32[]{:S(2)}) async-start(bf16[32,2,576]{2,1,0:T(2,128)(2,1)} %reshape.304), calls=%async_computation.6 | async-start | bytes 163840 | tf_op jit(solution)/shard_map/all_to_all | solution.py:40
  180.8 8.5 %copy-start.20 = (f32[256]{0:T(256)S(1)}, f32[256]{0:T(256)}, u32[]{:S(2)}) copy-start(f32[256]{0:T(256)} %copy-done.19) | copy-start | bytes 3076
  180.8 8.5 %copy-start.22 = (f32[64]{0:T(128)S(1)}, f32[64]{0:T(128)}, u32[]{:S(2)}) copy-start(f32[64]{0:T(128)} %copy-done.21) | copy-start | bytes 772
  180.8 8.5 %copy-start.25 = (f32[256]{0:T(256)S(1)}, f32[256]{0:T(256)}, u32[]{:S(2)}) copy-start(f32[256]{0:T(256)} %get-tuple-element.62) | copy-start | bytes 3076
  180.8 8.5 %copy-start.31 = (f32[64]{0:T(128)S(1)}, f32[64]{0:T(128)}, u32[]{:S(2)}) copy-start(f32[64]{0:T(128)} %get-tuple-element.67) | copy-start | bytes 772
  190.1 16.2 %all-to-all-start.8 = ((f32[16,1,2304]{2,1,0:T(1,128)}), f32[16,1,2304]{2,1,0:T(1,128)}, u32[]{:S(2)}, u32[]{:S(2)}) async-start(f32[16,1,2304]{2,1,0:T(1,128)} %broadcast_in_dim.23), calls=%async_computation.8 | async-start | bytes 294912 | tf_op jit(solution)/shard_map/all_to_all | solution.py:15
  (13 other events, 30.0 us)
where the time goes:
time: 259 us; the launch traced here: 258 us
  blocking collectives  107 us (41%)
  starting transfers between devices  50.4 us (19%)
  waiting for transfers between devices  29.7 us (11%)
  matrix products  27.6 us (11%)
  other arithmetic  25.9 us (10%)
  local copies, waits for them, and re-layouts  16.1 us (6%)
    all_to_all x4, blocking collectives, sent_to_all(): return lax.all_to_all(copies, axis, split_axis=0, concat_axis=0, tiled=True)  58.9 us
    all_gather x1, blocking collectives, gather_together(): lines, at, finished = (lax.all_gather(line, axis), 0, [])  47.8 us
    all_to_all x3, starting transfers between devices, sent_to_all(): return lax.all_to_all(copies, axis, split_axis=0, concat_axis=0, tiled=True)  18.7 us
    ppermute x4, starting transfers between devices, from_partner(): lax.ppermute(value, axis, [(i, i ^ 1 << distance) for i in range(lax.axis...  16.1 us
    all_to_all x3, waiting for transfers between devices, sent_to_all(): return lax.all_to_all(copies, axis, split_axis=0, concat_axis=0, tiled=True)  15.7 us
    all_to_all x2, starting transfers between devices, sum_at_owner(): lax.all_to_all(cut_along(value, dim, length), axis, 0, 0, tiled=True)  15.6 us
    dot_general x9, matrix products, kernel_grad(): jnp.einsum('nohw,nihw->oi', grad_conv_out, window, preferred_element_type...  9.19 us
    unnamed x80, local copies, waits for them, and re-layouts  8.59 us
  transfers between devices with their start and end apart: 9, of which 8 were waited for; matrix products, arithmetic and copies ran while one was open for 13% of the time, Pallas kernels for 0%

commit v1 on v0

v1 whole, which is shorter than its diff:
```python
import functools

import jax
import jax.numpy as jnp
from jax import lax
from jax.experimental import pallas as pl
from jax.experimental.pallas import tpu as pltpu
from jax.sharding import PartitionSpec as P

MESH = pl.DeviceIdType.MESH
F32 = jnp.float32
BF16 = jnp.bfloat16
EPS = 1e-05
LANES = 128


def dot(a, b):
    return lax.dot_general(a, b, (((1,), (0,)), ((), ())), preferred_element_type=F32)


def dot_nt(a, b):
    return lax.dot_general(a, b, (((1,), (1,)), ((), ())), preferred_element_type=F32)


def to_column(row):
    return jnp.transpose(jnp.broadcast_to(row, (LANES, LANES)))


def columns_of(rows, depth):
    parts = [to_column(rows[k : k + 1]) for k in range(rows.shape[0])]
    return jnp.concatenate(parts, axis=0)[:depth] if len(parts) > 1 else parts[0][:depth]


def put_rows(ref, first, second):
    depth = first.shape[0]
    blocks = ref.shape[0] // 2
    lane = lax.broadcasted_iota(jnp.int32, (depth, LANES), 1)
    table = jnp.where(lane == 0, first, jnp.where(lane == 1, second, 0.0))
    if depth < LANES:
        table = jnp.concatenate([table, jnp.zeros((LANES - depth, LANES), F32)], axis=0)
    for k in range(blocks):
        turned = jnp.transpose(table[k * LANES : (k + 1) * LANES])
        ref[k : k + 1, :] = turned[0:1]
        ref[blocks + k : blocks + k + 1, :] = turned[1:2]


def kernel(
    n_sp, n_bn, n_dp, per_image,
    img, cot, cw, pw, g1, b1, g3, b3,
    o_img, o_cw, o_pw, o_g1, o_b1, o_g3, o_b3,
    xin, gin, flat, gflat, xs, hid, slope, ybuf, wide, egrad, das, out,
    wfwd, wbwd, wproj, col_s, col_r, row_r, diag_r, row_s, dcol_s, dcol_r, drow_s, drow_r, ddiag_r,
    m1s, m1r, m3s, m3r, q3s, q3r, q1s, q1r, dw, pg, tiles, rtiles, dts, dtr, vs, vr, ags, agr, vec,
    co3, co1, rsem, ssem, lsem,
):
    C, TH, W = xin.shape
    CO = gin.shape[0]
    NG = n_sp * n_bn
    nb1, nb3 = m1s.shape[0] // 2, m3s.shape[0] // 2
    n_local = float(TH * W)
    M = n_local * NG
    sp, bn, dp = lax.axis_index("sp"), lax.axis_index("bn"), lax.axis_index("dp")
    me = sp * n_bn + bn
    column = lax.rem(sp, 2)
    rowhalf = sp // 2

    def peer(k):
        return (lax.rem(sp + k // n_bn, n_sp), lax.rem(bn + lax.rem(k, n_bn), n_bn), dp)

    def across(k):
        return (sp, bn, lax.rem(dp + k, n_dp))

    in_x = pltpu.make_async_copy(img.at[0, 0], xin, lsem.at[0])
    in_g = pltpu.make_async_copy(cot.at[0, 0], gin, lsem.at[1])
    in_x.start()
    in_g.start()

    barrier = pltpu.get_barrier_semaphore()

    def greet(k, carry):
        pl.semaphore_signal(barrier, inc=1, device_id=peer(k), device_id_type=MESH)
        return carry

    lax.fori_loop(1, NG, greet, 0)

    def greet_across(k, carry):
        pl.semaphore_signal(barrier, inc=1, device_id=across(k), device_id_type=MESH)
        return carry

    lax.fori_loop(1, n_dp, greet_across, 0)

    taps = [cw[n // 3, n % 3].astype(F32) for n in range(9)]
    wfwd[...] = jnp.concatenate(taps, axis=1).astype(BF16)
    flipped = jnp.concatenate([taps[8 - n] for n in range(9)], axis=0)
    wbwd[...] = jnp.transpose(flipped).astype(BF16)
    wproj[...] = jnp.transpose(pw[...].astype(F32)).astype(BF16)
    vec[...] = jnp.zeros_like(vec)
    vec[0:1, 0:C] = g1[...]
    vec[1:2, 0:C] = b1[...]
    vec[2 : 2 + nb3, :] = g3[...]
    vec[2 + nb3 : 2 + 2 * nb3, :] = b3[...]

    in_x.wait()

    def widen(c, carry):
        flat[pl.ds(pl.multiple_of(c * TH, 8), TH), :] = xin[c].astype(F32)
        return carry

    lax.fori_loop(0, C, widen, 0, unroll=4)

    lane = lax.broadcasted_iota(jnp.int32, (C, W), 1)
    edge_mine = jnp.where(column == 0, W - 1, 0)
    edge_other = (W - 1) - edge_mine
    row_mine = jnp.where(rowhalf == 0, TH - 1, 0)
    halo_row = jnp.where(rowhalf == 0, TH + 1, 0)
    empty_row = (TH + 1) - halo_row

    def pick(h):
        return flat[pl.ds(h, C, stride=TH), :]

    def gather_column(row_of):
        def step(h, packed):
            turned = pltpu.roll(row_of(h), lax.rem(h - edge_mine + W, W), 1)
            return jnp.where(lane == h, turned, packed)

        return lax.fori_loop(0, TH, step, jnp.zeros((C, W), F32), unroll=4)

    col_s[...] = gather_column(pick).astype(BF16)
    row_s[...] = pick(row_mine).astype(BF16)

    pl.semaphore_wait(barrier, NG - 1 + n_dp - 1)

    beside = (sp + 1 - 2 * column, bn, dp)
    below = (lax.rem(sp + 2, 4), bn, dp)
    corner = (3 - sp, bn, dp)

    def halo(cs, cr, rs, rr, dr, base):
        return [
            pltpu.make_async_remote_copy(cs, cr, ssem.at[base], rsem.at[base], device_id=beside, device_id_type=MESH),
            pltpu.make_async_remote_copy(
                rs, rr, ssem.at[base + 1], rsem.at[base + 1], device_id=below, device_id_type=MESH
            ),
            pltpu.make_async_remote_copy(
                rs, dr, ssem.at[base + 2], rsem.at[base + 2], device_id=corner, device_id_type=MESH
            ),
        ]

    x_halo = halo(col_s, col_r, row_s, row_r, diag_r, 0)
    for copy in x_halo:
        copy.start()

    in_g.wait()

    def widen_g(c, carry):
        gflat[pl.ds(pl.multiple_of(c * TH, 8), TH), :] = gin[c].astype(F32)
        return carry

    lax.fori_loop(0, CO, widen_g, 0, unroll=8)

    def shifted_rows(dst, r, row, side):
        left = jnp.where(lane == 0, jnp.where(column == 1, side, 0.0), pltpu.roll(row, 1, 1))
        right = jnp.where(lane == W - 1, jnp.where(column == 0, side, 0.0), pltpu.roll(row, W - 1, 1))
        dst[r, 0:C, :] = left.astype(BF16)
        dst[r, C : 2 * C, :] = row.astype(BF16)
        dst[r, 2 * C : 3 * C, :] = right.astype(BF16)

    def build(dst, row_of, cr, rr, dr):
        sides = cr[...].astype(F32)

        def step(h, carry):
            shifted_rows(dst, h + 1, row_of(h), pltpu.roll(sides, lax.rem(edge_mine - h + W, W), 1))
            return carry

        lax.fori_loop(0, TH, step, 0, unroll=2)
        dst[empty_row] = jnp.zeros((3 * C, W), BF16)
        shifted_rows(dst, halo_row, rr[...].astype(F32), pltpu.roll(dr[...].astype(F32), lax.rem(edge_mine - edge_other + W, W), 1))

    for copy in x_halo:
        copy.wait()
    build(xs, pick, col_r, row_r, diag_r)

    R = 4

    def stack(src, h):
        parts = [src[pl.ds(h + j, 3)].reshape(9 * C, W) for j in range(R)]
        return jnp.concatenate(parts, axis=1)

    def conv(p, carry):
        h = p * R
        block = dot(wfwd[...], stack(xs, h))
        for j in range(R):
            hid[h + j] = block[:, j * W : (j + 1) * W]
        return carry

    lax.fori_loop(0, TH // R, conv, 0)

    def exchange(src, dst, n):
        pltpu.make_async_copy(src, dst.at[me], rsem.at[n]).start()

        def send(k, carry):
            pltpu.make_async_remote_copy(
                src, dst.at[me], ssem.at[n], rsem.at[n], device_id=peer(k), device_id_type=MESH
            ).start()
            return carry

        lax.fori_loop(1, NG, send, 0)

    def arrived(dst, n):
        pltpu.make_async_copy(dst, dst, rsem.at[n]).wait()

    def moments(src, depth, message):
        chunk = min(depth, 64)
        firsts, seconds = [], []
        for c in range(0, depth, chunk):
            base = jnp.sum(src[0, c : c + chunk, :], axis=1, keepdims=True) * (1.0 / W)
            shift = jnp.broadcast_to(base, (chunk, W))

            def step(p, carry):
                total, squares = carry
                for j in range(4):
                    v = src[p * 4 + j, c : c + chunk, :] - shift
                    total = total + v
                    squares = squares + v * v
                return total, squares

            zero = jnp.zeros((chunk, W), F32)
            total, squares = lax.fori_loop(0, TH // 4, step, (zero, zero))
            local = jnp.sum(total, axis=1, keepdims=True)
            firsts.append(base + local * (1.0 / n_local))
            seconds.append(jnp.sum(squares, axis=1, keepdims=True) - local * local * (1.0 / n_local))
        put_rows(message, jnp.concatenate(firsts, axis=0), jnp.concatenate(seconds, axis=0))

    def combined(ref, blocks):
        means = ref[:, 0:blocks, :]
        mean = jnp.sum(means, axis=0) * (1.0 / NG)
        off = means - mean[None]
        total = jnp.sum(ref[:, blocks : 2 * blocks, :], axis=0) + n_local * jnp.sum(off * off, axis=0)
        return mean, lax.rsqrt(total * (1.0 / M) + EPS)

    moments(hid, C, m1s)
    exchange(m1s, m1r, 6)
    arrived(m1r, 6)
    mean1, scale1 = combined(m1r, nb1)
    gain1, bias1 = vec[0:1, :], vec[1:2, :]
    co1[0] = columns_of(0.5 * gain1 * scale1, C)
    co1[1] = columns_of(0.5 * (bias1 - mean1 * gain1 * scale1), C)

    def activate(p, carry):
        h = p * R
        rows = []
        for j in range(R):
            half = hid[h + j] * co1[0] + co1[1]
            t = jnp.tanh(half)
            u = 1.0 + t
            y = (half * u).astype(BF16)
            hid[h + j] = half
            slope[h + j] = 0.5 * u * (1.0 + half * (1.0 - t))
            ybuf[h + j] = y
            rows.append(y)
        block = dot(wproj[...], jnp.concatenate(rows, axis=1))
        for j in range(R):
            wide[h + j] = block[:, j * W : (j + 1) * W]
        return carry

    lax.fori_loop(0, TH // R, activate, 0)

    moments(wide, CO, m3s)
    exchange(m3s, m3r, 7)
    arrived(m3r, 7)
    mean3, scale3 = combined(m3r, nb3)
    gain3, bias3 = vec[2 : 2 + nb3, :], vec[2 + nb3 : 2 + 2 * nb3, :]
    co3[0] = columns_of(0.5 * gain3 * scale3, CO)
    co3[1] = columns_of(0.5 * (bias3 - mean3 * gain3 * scale3), CO)

    step_c = 32
    firsts, seconds = [], []
    for c in range(0, CO, step_c):
        alpha, beta = co3[0, c : c + step_c, :], co3[1, c : c + step_c, :]

        def slopes(p, carry):
            total, cross = carry
            for j in range(4):
                h = p * 4 + j
                half = wide[h, c : c + step_c, :] * alpha + beta
                t = jnp.tanh(half)
                g = gflat[pl.ds(c * TH + h, step_c, stride=TH), :]
                e = g * ((1.0 + t) * (1.0 + half * (1.0 - t)))
                wide[h, c : c + step_c, :] = half
                egrad[h, c : c + step_c, :] = e
                total = total + e
                cross = cross + e * half
            return total, cross

        zero = jnp.zeros((step_c, W), F32)
        total, cross = lax.fori_loop(0, TH // 4, slopes, (zero, zero))
        firsts.append(jnp.sum(total, axis=1, keepdims=True))
        seconds.append(jnp.sum(cross, axis=1, keepdims=True))
    put_rows(q3s, jnp.concatenate(firsts, axis=0), jnp.concatenate(seconds, axis=0))
    exchange(q3s, q3r, 8)
    arrived(q3r, 8)
    e_sum = jnp.sum(q3r[:, 0:nb3, :], axis=0)
    eh_sum = jnp.sum(q3r[:, nb3 : 2 * nb3, :], axis=0)
    s3 = 0.5 * e_sum
    q3 = (eh_sum - bias3 * s3) / gain3
    vs[...] = jnp.zeros_like(vs)
    vs[0:nb3, :] = s3
    vs[nb3 : 2 * nb3, :] = q3
    co3[0] = columns_of(0.5 * gain3 * scale3, CO)
    co3[1] = columns_of((-2.0 / M) * scale3 * q3, CO)
    co3[2] = columns_of((1.0 / M) * scale3 * (q3 * bias3 - gain3 * s3), CO)

    pg[...] = jnp.zeros_like(pg)

    def unproject(p, carry):
        total, cross = carry
        h = p * R
        rows = []
        for j in range(R):
            pieces = []
            for c in range(0, CO, 64):
                part = slice(c, c + 64)
                grad = egrad[h + j, part, :] * co3[0, part, :] + wide[h + j, part, :] * co3[1, part, :]
                pieces.append((grad + co3[2, part, :]).astype(BF16))
            rows.append(jnp.concatenate(pieces, axis=0))
        grads = jnp.concatenate(rows, axis=1)
        hidden = jnp.concatenate([ybuf[h + j] for j in range(R)], axis=1)
        pg[...] += dot_nt(hidden, grads)
        block = dot(pw[...], grads)
        for j in range(R):
            e = block[:, j * W : (j + 1) * W] * slope[h + j]
            slope[h + j] = e
            total = total + e
            cross = cross + e * hid[h + j]
        return total, cross

    zero = jnp.zeros((C, W), F32)
    total, cross = lax.fori_loop(0, TH // R, unproject, (zero, zero))
    put_rows(q1s, jnp.sum(total, axis=1, keepdims=True), jnp.sum(cross, axis=1, keepdims=True))
    exchange(q1s, q1r, 9)

    lt_c = dw.shape[1] // LANES
    lt_p = CO // LANES
    n_conv = C // 16 * lt_c
    n_tiles = n_conv + C // 16 * lt_p

    def scatter(low, high):
        def send(k, carry):
            to = peer(k)
            owner = to[0] * n_bn + to[1]

            @pl.when(jnp.logical_and(owner >= low, owner < high))
            def _():
                pltpu.make_async_remote_copy(
                    tiles.at[owner], rtiles.at[me], ssem.at[10], rsem.at[10], device_id=to, device_id_type=MESH
                ).start()

            return carry

        @pl.when(jnp.logical_and(me >= low, me < high))
        def _():
            pltpu.make_async_copy(tiles.at[me], rtiles.at[me], rsem.at[10]).start()

        lax.fori_loop(1, NG, send, 0)

    for r in range(C // 16):
        for t in range(lt_p):
            tiles[n_conv + r * lt_p + t] = pg[r * 16 : (r + 1) * 16, t * LANES : (t + 1) * LANES].astype(BF16)
    scatter(n_conv, n_tiles)

    arrived(q1r, 9)
    s1 = jnp.sum(q1r[:, 0:nb1, :], axis=0)
    eh1 = jnp.sum(q1r[:, nb1 : 2 * nb1, :], axis=0)
    safe = jnp.where(lax.broadcasted_iota(jnp.int32, (1, LANES), 1) < C, gain1, 1.0)
    q1 = (2.0 * eh1 - bias1 * s1) / safe
    vs[2 * nb3 : 2 * nb3 + 1, :] = s1
    vs[2 * nb3 + 1 : 2 * nb3 + 2, :] = q1
    co1[0] = columns_of(gain1 * scale1, C)
    co1[1] = columns_of((-2.0 / M) * scale1 * q1, C)
    co1[2] = columns_of((1.0 / M) * scale1 * (q1 * bias1 - gain1 * s1), C)

    def spread(src, dst, n):
        pltpu.make_async_copy(src, dst.at[dp], rsem.at[n]).start()

        def send(k, carry):
            pltpu.make_async_remote_copy(
                src, dst.at[dp], ssem.at[n], rsem.at[n], device_id=across(k), device_id_type=MESH
            ).start()
            return carry

        lax.fori_loop(1, n_dp, send, 0)

    spread(vs, vr, 11)

    def unnorm(h, packed):
        row = slope[h] * co1[0] + hid[h] * co1[1] + co1[2]
        slope[h] = row
        das[h + 1, C : 2 * C, :] = row.astype(BF16)
        turned = pltpu.roll(row, lax.rem(h - edge_mine + W, W), 1)
        return jnp.where(lane == h, turned, packed)

    dcol_s[...] = lax.fori_loop(0, TH, unnorm, jnp.zeros((C, W), F32), unroll=4).astype(BF16)
    drow_s[...] = slope[row_mine].astype(BF16)
    d_halo = halo(dcol_s, dcol_r, drow_s, drow_r, ddiag_r, 3)
    for copy in d_halo:
        copy.start()

    dw[...] = jnp.zeros_like(dw)

    def weigh(p, carry):
        h = p * R
        grads = jnp.concatenate([das[h + j + 1, C : 2 * C, :] for j in range(R)], axis=1)
        dw[:, 0 : 9 * C] += dot_nt(grads, stack(xs, h))
        return carry

    lax.fori_loop(0, TH // R, weigh, 0)
    for r in range(C // 16):
        for t in range(lt_c):
            tiles[r * lt_c + t] = dw[r * 16 : (r + 1) * 16, t * LANES : (t + 1) * LANES].astype(BF16)
    scatter(0, n_conv)

    for copy in d_halo:
        copy.wait()
    build(das, lambda h: slope[h], dcol_r, drow_r, ddiag_r)

    def unconv(p, carry):
        h = p * R
        block = dot(wbwd[...], stack(das, h))
        for j in range(R):
            flat[pl.ds(h + j, C, stride=TH), :] = block[:, j * W : (j + 1) * W]
        return carry

    lax.fori_loop(0, TH // R, unconv, 0)

    @pl.when(me < n_tiles)
    def _():
        arrived(rtiles, 10)
        dts[...] = jnp.sum(rtiles[...].astype(F32), axis=0).astype(BF16)
        spread(dts, dtr, 12)

    def narrow(c, carry):
        out[c] = flat[pl.ds(pl.multiple_of(c * TH, 8), TH), :].astype(BF16)
        return carry

    lax.fori_loop(0, C, narrow, 0, unroll=4)
    put = pltpu.make_async_copy(out, o_img.at[0, 0], lsem.at[2])
    put.start()

    @pl.when(me < n_tiles)
    def _():
        arrived(dtr, 12)
        ags[...] = (jnp.sum(dtr[...].astype(F32), axis=0) * per_image).astype(BF16)
        exchange(ags, agr, 13)

    arrived(vr, 11)
    sums = jnp.sum(vr[...], axis=0) * per_image
    o_b3[...] = sums[0:nb3]
    o_g3[...] = sums[nb3 : 2 * nb3]
    o_b1[...] = sums[2 * nb3 : 2 * nb3 + 1, 0:C]
    o_g1[...] = sums[2 * nb3 + 1 : 2 * nb3 + 2, 0:C]

    gathered = agr.at[pl.ds(0, n_tiles)]
    pltpu.make_async_copy(gathered, gathered, rsem.at[13]).wait()
    for r in range(C // 16):
        rows = slice(r * 16, (r + 1) * 16)
        for t in range(lt_p):
            o_pw[rows, t * LANES : (t + 1) * LANES] = agr[n_conv + r * lt_p + t].astype(F32)
        line = [agr[r * lt_c + t].astype(F32) for t in range(lt_c)]
        line = jnp.concatenate(line, axis=1)
        for n in range(9):
            o_cw[n // 3, n % 3, rows, :] = line[:, n * C : (n + 1) * C]

    for dst, n in ((m1r, 6), (m3r, 7), (q3r, 8), (q1r, 9)):
        sent = dst.at[pl.ds(0, NG - 1)]
        pltpu.make_async_copy(sent, sent, ssem.at[n]).wait()
    sent = vr.at[pl.ds(0, n_dp - 1)]
    pltpu.make_async_copy(sent, sent, ssem.at[11]).wait()

    @pl.when(me < n_tiles)
    def _():
        sent = tiles.at[pl.ds(0, n_tiles - 1)]
        pltpu.make_async_copy(sent, sent, ssem.at[10]).wait()
        sent = dtr.at[pl.ds(0, n_dp - 1)]
        pltpu.make_async_copy(sent, sent, ssem.at[12]).wait()
        sent = agr.at[pl.ds(0, NG - 1)]
        pltpu.make_async_copy(sent, sent, ssem.at[13]).wait()

    @pl.when(me >= n_tiles)
    def _():
        sent = tiles.at[pl.ds(0, n_tiles)]
        pltpu.make_async_copy(sent, sent, ssem.at[10]).wait()

    put.wait()


def solution(mesh):
    n_sp, n_bn, n_dp = mesh.shape["sp"], mesh.shape["bn"], mesh.shape["dp"]
    NG = n_sp * n_bn

    def step(images, out_grad, conv_weight, proj_weight, gain_one, shift_one, gain_three, shift_three):
        C, TH, W = images.shape[2:]
        CO = out_grad.shape[2]
        nb1, nb3 = 1, CO // LANES
        wide_c = -(-9 * C // LANES) * LANES
        n_tiles = C // 16 * (wide_c // LANES + CO // LANES)
        vm = pltpu.VMEM
        scratch = [
            vm((C, TH, W), BF16), vm((CO, TH, W), BF16), vm((C * TH, W), F32), vm((CO * TH, W), F32),
            vm((TH + 2, 3 * C, W), BF16), vm((TH, C, W), F32), vm((TH, C, W), F32), vm((TH, C, W), BF16),
            vm((TH, CO, W), F32), vm((TH, CO, W), F32), vm((TH + 2, 3 * C, W), BF16), vm((C, TH, W), BF16),
            vm((C, 9 * C), BF16), vm((C, 9 * C), BF16), vm((CO, C), BF16),
            *[vm((C, W), BF16) for _ in range(10)][:5], *[vm((C, W), BF16) for _ in range(5)],
            vm((2 * nb1, LANES), F32), vm((NG, 2 * nb1, LANES), F32),
            vm((2 * nb3, LANES), F32), vm((NG, 2 * nb3, LANES), F32),
            vm((2 * nb3, LANES), F32), vm((NG, 2 * nb3, LANES), F32),
            vm((2 * nb1, LANES), F32), vm((NG, 2 * nb1, LANES), F32),
            vm((C, wide_c), F32), vm((C, CO), F32), vm((n_tiles, 16, LANES), BF16), vm((NG, 16, LANES), BF16),
            vm((16, LANES), BF16), vm((n_dp, 16, LANES), BF16), vm((8, LANES), F32), vm((n_dp, 8, LANES), F32),
            vm((16, LANES), BF16), vm((NG, 16, LANES), BF16), vm((8, LANES), F32),
            vm((3, CO, W), F32), vm((3, C, W), F32),
            pltpu.SemaphoreType.DMA((14,)), pltpu.SemaphoreType.DMA((14,)), pltpu.SemaphoreType.DMA((3,)),
        ]
        vspec = pl.BlockSpec(memory_space=pltpu.VMEM)
        aspec = pl.BlockSpec(memory_space=pl.ANY)
        shape = jax.ShapeDtypeStruct
        got = pl.pallas_call(
            functools.partial(kernel, n_sp, n_bn, n_dp, 1.0 / float(n_sp * TH * W)),
            out_shape=(
                shape(images.shape, BF16), shape((3, 3, C, C), F32), shape((C, CO), F32), shape((1, C), F32),
                shape((1, C), F32), shape((nb3, LANES), F32), shape((nb3, LANES), F32),
            ),
            in_specs=[aspec, aspec] + [vspec] * 6,
            out_specs=(aspec,) + (vspec,) * 6,
            scratch_shapes=scratch,
            compiler_params=pltpu.CompilerParams(
                collective_id=0, has_side_effects=True, vmem_limit_bytes=60 * 1024 * 1024
            ),
        )(
            images, out_grad, conv_weight, proj_weight, gain_one.reshape(1, C), shift_one.reshape(1, C),
            gain_three.reshape(nb3, LANES), shift_three.reshape(nb3, LANES),
        )
        return (
            got[0], got[1], got[2], got[3].reshape(C), got[4].reshape(C), got[5].reshape(CO), got[6].reshape(CO),
        )

    split = P(("bn", "dp"), "sp", None, None, None)
    return jax.shard_map(
        step,
        mesh=mesh,
        in_specs=(split, split) + (P(),) * 6,
        out_specs=(split,) + (P(),) * 6,
        check_vma=False,
    )
```

time: 259 us -> 96.3 us (0.37)
  blocking collectives: 107 us -> 0 us
  Pallas kernels: 0 us -> 84.4 us
  starting transfers between devices: 50.4 us -> 0 us
  waiting for transfers between devices: 29.7 us -> 0 us
  matrix products: 27.6 us -> 0 us
  other arithmetic: 25.9 us -> 0 us
  local copies, waits for them, and re-layouts: 16.1 us -> 9.87 us
    pallas_call x0 -> x1, Pallas kernels: none -> 84.4 us  [step(): pl.pallas_call(functools.partial(kernel, n_sp, n_bn, n_dp, 1.0 / float(n_...]
    all_to_all x4 -> x0, blocking collectives: 58.9 us -> none  [sent_to_all(): return lax.all_to_all(copies, axis, split_axis=0, concat_axis=0, tiled=True)]
    all_gather x1 -> x0, blocking collectives: 47.8 us -> none  [gather_together(): lines, at, finished = (lax.all_gather(line, axis), 0, [])]
    all_to_all x5 -> x0, starting transfers between devices: 34.3 us -> none  [the longest x3 18.7 us: sent_to_all(): return lax.all_to_all(copies, axis, split_axis=0, concat_axis=0, tiled=True)]
    dot_general x30 -> x0, matrix products: 27.6 us -> none  [the longest x9 9.19 us: kernel_grad(): jnp.einsum('nohw,nihw->oi', grad_conv_out, window, preferred_element_type...]
    all_to_all x5 -> x0, waiting for transfers between devices: 22 us -> none  [the longest x3 15.7 us: sent_to_all(): return lax.all_to_all(copies, axis, split_axis=0, concat_axis=0, tiled=True)]
    ppermute x4 -> x0, starting transfers between devices: 16.1 us -> none  [from_partner(): lax.ppermute(value, axis, [(i, i ^ 1 << distance) for i in range(lax.axis...]
    reduce_sum x12 -> x0, other arithmetic: 9.55 us -> none  [the longest x1 4.68 us: norm_backward(): local_sum = jnp.sum(grad_pre, axis=(0, 2, 3))]
  transfers between devices with their start and end apart: 9 -> 0, of which waited for: 8 -> 0; matrix products, arithmetic and copies ran while one was open for 13% -> 0% of each run, Pallas kernels for 0% -> 0%
where the time goes in v1:
time: 96.3 us; the launch traced here: 95 us
  Pallas kernels  84.4 us (88%)
  local copies, waits for them, and re-layouts  9.87 us (10%)
    pallas_call x1, Pallas kernels, step(): pl.pallas_call(functools.partial(kernel, n_sp, n_bn, n_dp, 1.0 / float(n_...  84.4 us
    unnamed x7, local copies, waits for them, and re-layouts  9.87 us

profile of v1, /device:TPU:6, one launch (start us, length us, event | category | flops | bytes accessed | tf_op | source)
XLA Modules:
  0.0 95.0 jit_solution(14687545844852669784)
XLA Ops:
  0.6 84.4 %shard_map.135 = (bf16[1,1,64,40,128]{4,3,2,1,0:T(8,128)(2,1)}, f32[3,3,64,64]{3,2,1,0:T(8,128)}, f32[64,256]{1,0:T(8,128)}, f32[1,64]{1,0:T(1,128)}, f32[1,64]{...) custom-call(bf16[1,1,64,40,128]{4,3,2,1,0:T(8,128)(2,1)} %img.1, bf16[1,1,256,40,128]{4,3,2,1,0:T(8,128)(2,1)} %cot.1, ...), custom_call_target="tpu_custom_call" | custom-call | tf_op jit(solution)/shard_map/pallas_call | solution.py:525
  85.1 2.0 %copy.22 = bf16[1,1,64,40,128]{4,3,2,1,0:T(8,128)(2,1)} copy(bf16[1,1,64,40,128]{4,3,2,1,0:T(8,128)(2,1)} %get-tuple-element.28) | data formatting | bytes 1310720
  87.1 1.7 %copy.23 = f32[3,3,64,64]{3,2,1,0:T(8,128)} copy(f32[3,3,64,64]{3,2,1,0:T(8,128)} %get-tuple-element.29) | data formatting | bytes 294912
  88.8 1.5 %copy.24 = f32[64,256]{1,0:T(8,128)} copy(f32[64,256]{1,0:T(8,128)} %get-tuple-element.30) | data formatting | bytes 131072
  90.2 1.1 %copy.25 = f32[64]{0:T(128)} copy(f32[64]{0:T(128)} %bitcast.15) | data formatting | bytes 512
  91.4 1.1 %copy.26 = f32[64]{0:T(128)} copy(f32[64]{0:T(128)} %bitcast.14) | data formatting | bytes 512
  92.5 1.2 %copy.27 = f32[256]{0:T(256)} copy(f32[256]{0:T(256)} %bitcast.11) | data formatting | bytes 2048
  93.7 1.2 %copy.28 = f32[256]{0:T(256)} copy(f32[256]{0:T(256)} %bitcast.10) | data formatting | bytes 2048

commit v2 on v1

--- a/solution.py
+++ b/solution.py
@@ -47,11 +47,11 @@
 def kernel(
     n_sp, n_bn, n_dp, per_image,
     img, cot, cw, pw, g1, b1, g3, b3,
-    o_img, o_cw, o_pw, o_g1, o_b1, o_g3, o_b3,
+    o_img, o_agr, o_sums,
     xin, gin, flat, gflat, xs, hid, slope, ybuf, wide, egrad, das, out,
     wfwd, wbwd, wproj, col_s, col_r, row_r, diag_r, row_s, dcol_s, dcol_r, drow_s, drow_r, ddiag_r,
     m1s, m1r, m3s, m3r, q3s, q3r, q1s, q1r, dw, pg, tiles, rtiles, dts, dtr, vs, vr, ags, agr, vec,
-    co3, co1, rsem, ssem, lsem,
+    co3, co1, dh, htiles, rhtiles, rsem, ssem, lsem,
 ):
     C, TH, W = xin.shape
     CO = gin.shape[0]
@@ -64,11 +64,25 @@
     column = lax.rem(sp, 2)
     rowhalf = sp // 2
 
+    def wrapped(at, step, size):
+        moved = at + step
+        return jnp.where(moved >= size, moved - size, moved)
+
+    xs_of = [wrapped(sp, k, n_sp) for k in range(n_sp)]
+    zs_of = [wrapped(bn, k, n_bn) for k in range(n_bn)]
+    ds_of = [wrapped(dp, k, n_dp) for k in range(n_dp)]
+
+    def ring(step, size):
+        return min(step, size - step)
+
+    peers = sorted(range(1, NG), key=lambda k: -ring(k // n_bn, n_sp) - ring(k % n_bn, n_bn))
+    others = sorted(range(1, n_dp), key=lambda k: -ring(k // 2, n_dp // 2))
+
     def peer(k):
-        return (lax.rem(sp + k // n_bn, n_sp), lax.rem(bn + lax.rem(k, n_bn), n_bn), dp)
+        return (xs_of[k // n_bn], zs_of[k % n_bn], dp)
 
     def across(k):
-        return (sp, bn, lax.rem(dp + k, n_dp))
+        return (sp, bn, ds_of[k])
 
     in_x = pltpu.make_async_copy(img.at[0, 0], xin, lsem.at[0])
     in_g = pltpu.make_async_copy(cot.at[0, 0], gin, lsem.at[1])
@@ -77,17 +91,10 @@
 
     barrier = pltpu.get_barrier_semaphore()
 
-    def greet(k, carry):
+    for k in peers:
         pl.semaphore_signal(barrier, inc=1, device_id=peer(k), device_id_type=MESH)
-        return carry
-
-    lax.fori_loop(1, NG, greet, 0)
-
-    def greet_across(k, carry):
+    for k in others:
         pl.semaphore_signal(barrier, inc=1, device_id=across(k), device_id_type=MESH)
-        return carry
-
-    lax.fori_loop(1, n_dp, greet_across, 0)
 
     taps = [cw[n // 3, n % 3].astype(F32) for n in range(9)]
     wfwd[...] = jnp.concatenate(taps, axis=1).astype(BF16)
@@ -128,6 +135,20 @@
     col_s[...] = gather_column(pick).astype(BF16)
     row_s[...] = pick(row_mine).astype(BF16)
 
+    def build(dst, h, row):
+        left = jnp.where(lane == 0, 0.0, pltpu.roll(row, 1, 1))
+        right = jnp.where(lane == W - 1, 0.0, pltpu.roll(row, W - 1, 1))
+        dst[h + 1, 0:C, :] = left.astype(BF16)
+        dst[h + 1, C : 2 * C, :] = row.astype(BF16)
+        dst[h + 1, 2 * C : 3 * C, :] = right.astype(BF16)
+
+    def lay_out(h, carry):
+        build(xs, h, pick(h))
+        return carry
+
+    lax.fori_loop(0, TH, lay_out, 0, unroll=4)
+    xs[empty_row] = jnp.zeros((3 * C, W), BF16)
+
     pl.semaphore_wait(barrier, NG - 1 + n_dp - 1)
 
     beside = (sp + 1 - 2 * column, bn, dp)
@@ -157,27 +178,25 @@
 
     lax.fori_loop(0, CO, widen_g, 0, unroll=8)
 
-    def shifted_rows(dst, r, row, side):
-        left = jnp.where(lane == 0, jnp.where(column == 1, side, 0.0), pltpu.roll(row, 1, 1))
-        right = jnp.where(lane == W - 1, jnp.where(column == 0, side, 0.0), pltpu.roll(row, W - 1, 1))
-        dst[r, 0:C, :] = left.astype(BF16)
-        dst[r, C : 2 * C, :] = row.astype(BF16)
-        dst[r, 2 * C : 3 * C, :] = right.astype(BF16)
-
-    def build(dst, row_of, cr, rr, dr):
+    inner = pl.ds(pl.multiple_of(jnp.where(column == 0, 2 * C, 0), 16), C)
+
+    def patch(dst, cr, rr, dr):
         sides = cr[...].astype(F32)
 
         def step(h, carry):
-            shifted_rows(dst, h + 1, row_of(h), pltpu.roll(sides, lax.rem(edge_mine - h + W, W), 1))
+            side = pltpu.roll(sides, lax.rem(edge_mine - h + W, W), 1)
+            dst[h + 1, inner, :] = jnp.where(lane == edge_mine, side, dst[h + 1, inner, :].astype(F32)).astype(BF16)
             return carry
 
-        lax.fori_loop(0, TH, step, 0, unroll=2)
-        dst[empty_row] = jnp.zeros((3 * C, W), BF16)
-        shifted_rows(dst, halo_row, rr[...].astype(F32), pltpu.roll(dr[...].astype(F32), lax.rem(edge_mine - edge_other + W, W), 1))
+        lax.fori_loop(0, TH, step, 0, unroll=4)
+        build(dst, halo_row - 1, rr[...].astype(F32))
+        side = pltpu.roll(dr[...].astype(F32), lax.rem(edge_mine - edge_other + W, W), 1)
+        held = dst[halo_row, inner, :].astype(F32)
+        dst[halo_row, inner, :] = jnp.where(lane == edge_mine, side, held).astype(BF16)
 
     for copy in x_halo:
         copy.wait()
-    build(xs, pick, col_r, row_r, diag_r)
+    patch(xs, col_r, row_r, diag_r)
 
     R = 4
 
@@ -197,13 +216,10 @@
     def exchange(src, dst, n):
         pltpu.make_async_copy(src, dst.at[me], rsem.at[n]).start()
 
-        def send(k, carry):
+        for k in peers:
             pltpu.make_async_remote_copy(
                 src, dst.at[me], ssem.at[n], rsem.at[n], device_id=peer(k), device_id_type=MESH
             ).start()
-            return carry
-
-        lax.fori_loop(1, NG, send, 0)
 
     def arrived(dst, n):
         pltpu.make_async_copy(dst, dst, rsem.at[n]).wait()
@@ -239,6 +255,13 @@
 
     moments(hid, C, m1s)
     exchange(m1s, m1r, 6)
+
+    def lay_out_g(h, carry):
+        for c in range(0, CO, 32):
+            egrad[h, c : c + 32, :] = gflat[pl.ds(c * TH + h, 32, stride=TH), :]
+        return carry
+
+    lax.fori_loop(0, TH, lay_out_g, 0)
     arrived(m1r, 6)
     mean1, scale1 = combined(m1r, nb1)
     gain1, bias1 = vec[0:1, :], vec[1:2, :]
@@ -266,6 +289,46 @@
 
     moments(wide, CO, m3s)
     exchange(m3s, m3r, 7)
+
+    lt_c = dw.shape[1] // LANES
+    lt_p = CO // LANES
+    n_conv = C // 16 * lt_c
+    n_tiles = n_conv + C // 16 * lt_p
+
+    def scatter(src, dst, low, high, n):
+        def send(to):
+            owner = to[0] * n_bn + to[1]
+
+            @pl.when(jnp.logical_and(owner >= low, owner < high))
+            def _():
+                pltpu.make_async_remote_copy(
+                    src.at[owner], dst.at[me], ssem.at[n], rsem.at[n], device_id=to, device_id_type=MESH
+                ).start()
+
+        @pl.when(jnp.logical_and(me >= low, me < high))
+        def _():
+            pltpu.make_async_copy(src.at[me], dst.at[me], rsem.at[n]).start()
+
+        for k in peers:
+            send(peer(k))
+
+    dh[...] = jnp.zeros_like(dh)
+
+    def weigh(p, carry):
+        h = p * R
+        ones = jnp.ones((16, W), BF16)
+        rows = [jnp.concatenate([hid[h + j].astype(BF16), ones], axis=0) for j in range(R)]
+        dh[:, 0 : 9 * C] += dot_nt(jnp.concatenate(rows, axis=1), stack(xs, h))
+        return carry
+
+    lax.fori_loop(0, TH // R, weigh, 0)
+    for r in range(C // 16):
+        for t in range(lt_c):
+            cols = slice(t * LANES, (t + 1) * LANES)
+            htiles[r * lt_c + t, 0:16, :] = dh[r * 16 : (r + 1) * 16, cols]
+            htiles[r * lt_c + t, 16:24, :] = dh[C : C + 8, cols]
+    scatter(htiles, rhtiles, 0, n_conv, 14)
+
     arrived(m3r, 7)
     mean3, scale3 = combined(m3r, nb3)
     gain3, bias3 = vec[2 : 2 + nb3, :], vec[2 + nb3 : 2 + 2 * nb3, :]
@@ -283,7 +346,7 @@
                 h = p * 4 + j
                 half = wide[h, c : c + step_c, :] * alpha + beta
                 t = jnp.tanh(half)
-                g = gflat[pl.ds(c * TH + h, step_c, stride=TH), :]
+                g = egrad[h, c : c + step_c, :]
                 e = g * ((1.0 + t) * (1.0 + half * (1.0 - t)))
                 wide[h, c : c + step_c, :] = half
                 egrad[h, c : c + step_c, :] = e
@@ -310,6 +373,7 @@
     co3[2] = columns_of((1.0 / M) * scale3 * (q3 * bias3 - gain3 * s3), CO)
 
     pg[...] = jnp.zeros_like(pg)
+    dw[...] = jnp.zeros_like(dw)
 
     def unproject(p, carry):
         total, cross = carry
@@ -326,46 +390,27 @@
         hidden = jnp.concatenate([ybuf[h + j] for j in range(R)], axis=1)
         pg[...] += dot_nt(hidden, grads)
         block = dot(pw[...], grads)
+        rows = []
         for j in range(R):
             e = block[:, j * W : (j + 1) * W] * slope[h + j]
             slope[h + j] = e
+            rows.append(e.astype(BF16))
             total = total + e
             cross = cross + e * hid[h + j]
+        dw[:, 0 : 9 * C] += dot_nt(jnp.concatenate(rows, axis=1), stack(xs, h))
         return total, cross
 
     zero = jnp.zeros((C, W), F32)
     total, cross = lax.fori_loop(0, TH // R, unproject, (zero, zero))
+    for r in range(C // 16):
+        rows = slice(r * 16, (r + 1) * 16)
+        for t in range(lt_c):
+            tiles[r * lt_c + t] = dw[rows, t * LANES : (t + 1) * LANES]
+        for t in range(lt_p):
+            tiles[n_conv + r * lt_p + t] = pg[rows, t * LANES : (t + 1) * LANES]
     put_rows(q1s, jnp.sum(total, axis=1, keepdims=True), jnp.sum(cross, axis=1, keepdims=True))
     exchange(q1s, q1r, 9)
-
-    lt_c = dw.shape[1] // LANES
-    lt_p = CO // LANES
-    n_conv = C // 16 * lt_c
-    n_tiles = n_conv + C // 16 * lt_p
-
-    def scatter(low, high):
-        def send(k, carry):
-            to = peer(k)
-            owner = to[0] * n_bn + to[1]
-
-            @pl.when(jnp.logical_and(owner >= low, owner < high))
-            def _():
-                pltpu.make_async_remote_copy(
-                    tiles.at[owner], rtiles.at[me], ssem.at[10], rsem.at[10], device_id=to, device_id_type=MESH
-                ).start()
-
-            return carry
-
-        @pl.when(jnp.logical_and(me >= low, me < high))
-        def _():
-            pltpu.make_async_copy(tiles.at[me], rtiles.at[me], rsem.at[10]).start()
-
-        lax.fori_loop(1, NG, send, 0)
-
-    for r in range(C // 16):
-        for t in range(lt_p):
-            tiles[n_conv + r * lt_p + t] = pg[r * 16 : (r + 1) * 16, t * LANES : (t + 1) * LANES].astype(BF16)
-    scatter(n_conv, n_tiles)
+    scatter(tiles, rtiles, 0, n_tiles, 10)
 
     arrived(q1r, 9)
     s1 = jnp.sum(q1r[:, 0:nb1, :], axis=0)
@@ -381,20 +426,17 @@
     def spread(src, dst, n):
         pltpu.make_async_copy(src, dst.at[dp], rsem.at[n]).start()
 
-        def send(k, carry):
+        for k in others:
             pltpu.make_async_remote_copy(
                 src, dst.at[dp], ssem.at[n], rsem.at[n], device_id=across(k), device_id_type=MESH
             ).start()
-            return carry
-
-        lax.fori_loop(1, n_dp, send, 0)
 
     spread(vs, vr, 11)
 
     def unnorm(h, packed):
         row = slope[h] * co1[0] + hid[h] * co1[1] + co1[2]
         slope[h] = row
-        das[h + 1, C : 2 * C, :] = row.astype(BF16)
+        build(das, h, row)
         turned = pltpu.roll(row, lax.rem(h - edge_mine + W, W), 1)
         return jnp.where(lane == h, turned, packed)
 
@@ -404,23 +446,30 @@
     for copy in d_halo:
         copy.start()
 
-    dw[...] = jnp.zeros_like(dw)
-
-    def weigh(p, carry):
-        h = p * R
-        grads = jnp.concatenate([das[h + j + 1, C : 2 * C, :] for j in range(R)], axis=1)
-        dw[:, 0 : 9 * C] += dot_nt(grads, stack(xs, h))
-        return carry
-
-    lax.fori_loop(0, TH // R, weigh, 0)
-    for r in range(C // 16):
-        for t in range(lt_c):
-            tiles[r * lt_c + t] = dw[r * 16 : (r + 1) * 16, t * LANES : (t + 1) * LANES].astype(BF16)
-    scatter(0, n_conv)
+    das[empty_row] = jnp.zeros((3 * C, W), BF16)
+
+    @pl.when(me < n_conv)
+    def _():
+        arrived(rhtiles, 14)
+        arrived(rtiles, 10)
+        rows = pl.ds(pl.multiple_of((me // lt_c) * 16, 16), 16)
+        whole = jnp.sum(rtiles[...], axis=0) * co1[0, rows, :]
+        whole = whole + jnp.sum(rhtiles[:, 0:16, :], axis=0) * co1[1, rows, :]
+        whole = whole + jnp.sum(rhtiles[:, 16:17, :], axis=0) * co1[2, rows, :]
+        dts[...] = whole.astype(BF16)
+
+    @pl.when(jnp.logical_and(me >= n_conv, me < n_tiles))
+    def _():
+        arrived(rtiles, 10)
+        dts[...] = jnp.sum(rtiles[...], axis=0).astype(BF16)
+
+    @pl.when(me < n_tiles)
+    def _():
+        spread(dts, dtr, 12)
 
     for copy in d_halo:
         copy.wait()
-    build(das, lambda h: slope[h], dcol_r, drow_r, ddiag_r)
+    patch(das, dcol_r, drow_r, ddiag_r)
 
     def unconv(p, carry):
         h = p * R
@@ -431,12 +480,6 @@
 
     lax.fori_loop(0, TH // R, unconv, 0)
 
-    @pl.when(me < n_tiles)
-    def _():
-        arrived(rtiles, 10)
-        dts[...] = jnp.sum(rtiles[...].astype(F32), axis=0).astype(BF16)
-        spread(dts, dtr, 12)
-
     def narrow(c, carry):
         out[c] = flat[pl.ds(pl.multiple_of(c * TH, 8), TH), :].astype(BF16)
         return carry
@@ -452,14 +495,57 @@
         exchange(ags, agr, 13)
 
     arrived(vr, 11)
-    sums = jnp.sum(vr[...], axis=0) * per_image
+    o_sums[...] = jnp.sum(vr[...], axis=0) * per_image
+
+    gathered = agr.at[pl.ds(0, n_tiles)]
+    pltpu.make_async_copy(gathered, gathered, rsem.at[13]).wait()
+    o_agr[...] = agr[0:n_tiles]
+
+    for dst, n in ((m1r, 6), (m3r, 7), (q3r, 8), (q1r, 9)):
+        sent = dst.at[pl.ds(0, NG - 1)]
+        pltpu.make_async_copy(sent, sent, ssem.at[n]).wait()
+    sent = vr.at[pl.ds(0, n_dp - 1)]
+    pltpu.make_async_copy(sent, sent, ssem.at[11]).wait()
+
+    @pl.when(me < n_tiles)
+    def _():
+        sent = rtiles.at[pl.ds(0, n_tiles - 1)]
+        pltpu.make_async_copy(sent, sent, ssem.at[10]).wait()
+        sent = dtr.at[pl.ds(0, n_dp - 1)]
+        pltpu.make_async_copy(sent, sent, ssem.at[12]).wait()
+        sent = agr.at[pl.ds(0, NG - 1)]
+        pltpu.make_async_copy(sent, sent, ssem.at[13]).wait()
+
+    @pl.when(me >= n_tiles)
+    def _():
+        sent = rtiles.at[pl.ds(0, n_tiles)]
+        pltpu.make_async_copy(sent, sent, ssem.at[10]).wait()
+
+    @pl.when(me < n_conv)
+    def _():
+        sent = rhtiles.at[pl.ds(0, n_conv - 1)]
+        pltpu.make_async_copy(sent, sent, ssem.at[14]).wait()
+
+    @pl.when(me >= n_conv)
+    def _():
+        sent = rhtiles.at[pl.ds(0, n_conv)]
+        pltpu.make_async_copy(sent, sent, ssem.at[14]).wait()
+
+    put.wait()
+
+
+def finish(img, agr, sums, o_img, o_cw, o_pw, o_g1, o_b1, o_g3, o_b3, sem):
+    copy = pltpu.make_async_copy(img, o_img, sem)
+    copy.start()
+    C = o_pw.shape[0]
+    nb3 = o_g3.shape[0]
+    lt_p = o_pw.shape[1] // LANES
+    lt_c = -(-9 * C // LANES)
+    n_conv = C // 16 * lt_c
     o_b3[...] = sums[0:nb3]
     o_g3[...] = sums[nb3 : 2 * nb3]
     o_b1[...] = sums[2 * nb3 : 2 * nb3 + 1, 0:C]
     o_g1[...] = sums[2 * nb3 + 1 : 2 * nb3 + 2, 0:C]
-
-    gathered = agr.at[pl.ds(0, n_tiles)]
-    pltpu.make_async_copy(gathered, gathered, rsem.at[13]).wait()
     for r in range(C // 16):
         rows = slice(r * 16, (r + 1) * 16)
         for t in range(lt_p):
@@ -468,28 +554,7 @@
         line = jnp.concatenate(line, axis=1)
         for n in range(9):
             o_cw[n // 3, n % 3, rows, :] = line[:, n * C : (n + 1) * C]
-
-    for dst, n in ((m1r, 6), (m3r, 7), (q3r, 8), (q1r, 9)):
-        sent = dst.at[pl.ds(0, NG - 1)]
-        pltpu.make_async_copy(sent, sent, ssem.at[n]).wait()
-    sent = vr.at[pl.ds(0, n_dp - 1)]
-    pltpu.make_async_copy(sent, sent, ssem.at[11]).wait()
-
-    @pl.when(me < n_tiles)
-    def _():
-        sent = tiles.at[pl.ds(0, n_tiles - 1)]
-        pltpu.make_async_copy(sent, sent, ssem.at[10]).wait()
-        sent = dtr.at[pl.ds(0, n_dp - 1)]
-        pltpu.make_async_copy(sent, sent, ssem.at[12]).wait()
-        sent = agr.at[pl.ds(0, NG - 1)]
-        pltpu.make_async_copy(sent, sent, ssem.at[13]).wait()
-
-    @pl.when(me >= n_tiles)
-    def _():
-        sent = tiles.at[pl.ds(0, n_tiles)]
-        pltpu.make_async_copy(sent, sent, ssem.at[10]).wait()
-
-    put.wait()
+    copy.wait()
 
 
 def solution(mesh):
@@ -501,7 +566,8 @@
         CO = out_grad.shape[2]
         nb1, nb3 = 1, CO // LANES
         wide_c = -(-9 * C // LANES) * LANES
-        n_tiles = C // 16 * (wide_c // LANES + CO // LANES)
+        n_conv = C // 16 * (wide_c // LANES)
+        n_tiles = n_conv + C // 16 * (CO // LANES)
         vm = pltpu.VMEM
         scratch = [
             vm((C, TH, W), BF16), vm((CO, TH, W), BF16), vm((C * TH, W), F32), vm((CO * TH, W), F32),
@@ -513,31 +579,41 @@
             vm((2 * nb3, LANES), F32), vm((NG, 2 * nb3, LANES), F32),
             vm((2 * nb3, LANES), F32), vm((NG, 2 * nb3, LANES), F32),
             vm((2 * nb1, LANES), F32), vm((NG, 2 * nb1, LANES), F32),
-            vm((C, wide_c), F32), vm((C, CO), F32), vm((n_tiles, 16, LANES), BF16), vm((NG, 16, LANES), BF16),
+            vm((C, wide_c), F32), vm((C, CO), F32), vm((n_tiles, 16, LANES), F32), vm((NG, 16, LANES), F32),
             vm((16, LANES), BF16), vm((n_dp, 16, LANES), BF16), vm((8, LANES), F32), vm((n_dp, 8, LANES), F32),
             vm((16, LANES), BF16), vm((NG, 16, LANES), BF16), vm((8, LANES), F32),
             vm((3, CO, W), F32), vm((3, C, W), F32),
-            pltpu.SemaphoreType.DMA((14,)), pltpu.SemaphoreType.DMA((14,)), pltpu.SemaphoreType.DMA((3,)),
+            vm((C + 16, wide_c), F32), vm((n_conv, 24, LANES), F32), vm((NG, 24, LANES), F32),
+            pltpu.SemaphoreType.DMA((15,)), pltpu.SemaphoreType.DMA((15,)), pltpu.SemaphoreType.DMA((3,)),
         ]
         vspec = pl.BlockSpec(memory_space=pltpu.VMEM)
         aspec = pl.BlockSpec(memory_space=pl.ANY)
+        hspec = pl.BlockSpec(memory_space=pltpu.HBM)
         shape = jax.ShapeDtypeStruct
-        got = pl.pallas_call(
+        img, tiles, sums = pl.pallas_call(
             functools.partial(kernel, n_sp, n_bn, n_dp, 1.0 / float(n_sp * TH * W)),
-            out_shape=(
-                shape(images.shape, BF16), shape((3, 3, C, C), F32), shape((C, CO), F32), shape((1, C), F32),
-                shape((1, C), F32), shape((nb3, LANES), F32), shape((nb3, LANES), F32),
-            ),
-            in_specs=[aspec, aspec] + [vspec] * 6,
-            out_specs=(aspec,) + (vspec,) * 6,
+            out_shape=(shape(images.shape, BF16), shape((n_tiles, 16, LANES), BF16), shape((8, LANES), F32)),
+            in_specs=[hspec, hspec] + [vspec] * 6,
+            out_specs=(aspec, vspec, vspec),
             scratch_shapes=scratch,
             compiler_params=pltpu.CompilerParams(
-                collective_id=0, has_side_effects=True, vmem_limit_bytes=60 * 1024 * 1024
+                collective_id=0, has_side_effects=True, vmem_limit_bytes=55200000
             ),
         )(
             images, out_grad, conv_weight, proj_weight, gain_one.reshape(1, C), shift_one.reshape(1, C),
             gain_three.reshape(nb3, LANES), shift_three.reshape(nb3, LANES),
         )
+        got = pl.pallas_call(
+            finish,
+            out_shape=(
+                shape(images.shape, BF16), shape((3, 3, C, C), F32), shape((C, CO), F32), shape((1, C), F32),
+                shape((1, C), F32), shape((nb3, LANES), F32), shape((nb3, LANES), F32),
+            ),
+            in_specs=[aspec, vspec, vspec],
+            out_specs=(aspec,) + (vspec,) * 6,
+            scratch_shapes=[pltpu.SemaphoreType.DMA],
+            compiler_params=pltpu.CompilerParams(vmem_limit_bytes=4 * 1024 * 1024),
+        )(img, tiles, sums)
         return (
             got[0], got[1], got[2], got[3].reshape(C), got[4].reshape(C), got[5].reshape(CO), got[6].reshape(CO),
         )

time: 96.3 us -> 79.6 us (0.83)
  Pallas kernels: 84.4 us -> 73.8 us
  local copies, waits for them, and re-layouts: 9.87 us -> 4.33 us
    pallas_call x1, Pallas kernels: 84.4 us -> 72.2 us  [step(): pl.pallas_call(functools.partial(kernel, n_sp, n_bn, n_dp, 1.0 / float(n_...]
    unnamed x7 -> x12, local copies, waits for them, and re-layouts: 9.87 us -> 4.33 us
    pallas_call x0 -> x1, Pallas kernels: none -> 1.6 us  [step(): pl.pallas_call(finish, out_shape=(shape(images.shape, BF16), shape((3, 3,...]
where the time goes in v2:
time: 79.6 us; the launch traced here: 78.8 us
  Pallas kernels  73.8 us (93%)
  local copies, waits for them, and re-layouts  4.33 us (5%)
    pallas_call x1, Pallas kernels, step(): pl.pallas_call(functools.partial(kernel, n_sp, n_bn, n_dp, 1.0 / float(n_...  72.2 us
    unnamed x12, local copies, waits for them, and re-layouts  4.33 us
    pallas_call x1, Pallas kernels, step(): pl.pallas_call(finish, out_shape=(shape(images.shape, BF16), shape((3, 3,...  1.6 us

profile of v2, /device:TPU:6, one launch (start us, length us, event | category | flops | bytes accessed | tf_op | source)
XLA Modules:
  0.0 78.8 jit_solution(17286004309547326238)
XLA Ops:
  0.6 0.0 copy-start
  0.6 0.9 %copy-done = bf16[3,3,64,64]{3,2,1,0:T(8,128)(2,1)S(1)} copy-done((bf16[3,3,64,64]{3,2,1,0:T(8,128)(2,1)S(1)}, bf16[3,3,64,64]{3,2,1,0:T(8,128)(2,1)}, u32[]{:S(2)}) %copy-start) | copy-done | bytes 73752
  1.5 0.0 copy-start.1
  1.5 0.8 copy-done.1
  2.3 0.0 copy-start.2
  2.3 0.7 copy-done.2
  3.0 0.0 copy-start.3
  3.0 0.7 copy-done.3
  3.7 0.0 copy-start.4
  3.7 0.7 copy-done.4
  4.3 0.0 copy-start.5
  4.3 0.7 copy-done.5
  5.0 72.2 %shard_map.135 = (bf16[1,1,64,40,128]{4,3,2,1,0:T(8,128)(2,1)S(1)}, bf16[28,16,128]{2,1,0:T(8,128)(2,1)S(1)}, f32[8,128]{1,0:T(8,128)S(1)}) custom-call(bf16[1,1,64,40,128]{4,3,2,1,0:T(8,128)(2,1)} %img.1, bf16[1,1,256,40,128]{4,3,2,1,0:T(8,128)(2,1)} %cot.1, bf16[3,3,64,64]{3,2,1,0:T(8,128)(2,1)S(1)} %copy-done, bf16[64,256]{1,0:T(8,128)(2,1)S(1)} %copy-done.1, ...), custom_call_target="tpu_custom_call" | custom-call | tf_op jit(solution)/shard_map/pallas_call | solution.py:593
  77.2 1.6 %shard_map.136 = (bf16[1,1,64,40,128]{4,3,2,1,0:T(8,128)(2,1)}, f32[3,3,64,64]{3,2,1,0:T(8,128)}, f32[64,256]{1,0:T(8,128)}, f32[1,64]{1,0:T(1,128)}, f32[1,64]{...) custom-call(bf16[1,1,64,40,128]{4,3,2,1,0:T(8,128)(2,1)S(1)} %get-tuple-element.17.img, ...), custom_call_target="tpu_custom_call" | custom-call | tf_op jit(solution)/shard_map/pallas_call | solution.py:606
Async XLA Ops:
  0.6 0.9 %copy-start = (bf16[3,3,64,64]{3,2,1,0:T(8,128)(2,1)S(1)}, bf16[3,3,64,64]{3,2,1,0:T(8,128)(2,1)}, u32[]{:S(2)}) copy-start(bf16[3,3,64,64]{3,2,1,0:T(8,128)(2,1)} %cw.1) | copy-start | bytes 221188
  1.5 0.8 copy-start.1
  2.3 0.7 copy-start.2
  3.0 0.7 copy-start.3
  3.7 0.7 copy-start.4
  4.3 0.7 copy-start.5

commit v3 on v2

--- a/solution.py
+++ b/solution.py
@@ -46,12 +46,13 @@
 
 def kernel(
     n_sp, n_bn, n_dp, per_image,
-    img, cot, cw, pw, g1, b1, g3, b3,
+    img, cot, cw_in, pw_in, g1_in, b1_in, g3_in, b3_in,
     o_img, o_agr, o_sums,
     xin, gin, flat, gflat, xs, hid, slope, ybuf, wide, egrad, das, out,
     wfwd, wbwd, wproj, col_s, col_r, row_r, diag_r, row_s, dcol_s, dcol_r, drow_s, drow_r, ddiag_r,
     m1s, m1r, m3s, m3r, q3s, q3r, q1s, q1r, dw, pg, tiles, rtiles, dts, dtr, vs, vr, ags, agr, vec,
-    co3, co1, dh, htiles, rhtiles, rsem, ssem, lsem,
+    co3, co1, dh, htiles, rhtiles, gram, ebuf,
+    cw, pw, g1, b1, g3, b3, rsem, ssem, lsem,
 ):
     C, TH, W = xin.shape
     CO = gin.shape[0]
@@ -86,7 +87,11 @@
 
     in_x = pltpu.make_async_copy(img.at[0, 0], xin, lsem.at[0])
     in_g = pltpu.make_async_copy(cot.at[0, 0], gin, lsem.at[1])
+    pairs = ((cw_in, cw), (pw_in, pw), (g1_in, g1), (b1_in, b1), (g3_in, g3), (b3_in, b3))
+    small = [pltpu.make_async_copy(src, dst, lsem.at[3 + i]) for i, (src, dst) in enumerate(pairs)]
     in_x.start()
+    for copy in small:
+        copy.start()
     in_g.start()
 
     barrier = pltpu.get_barrier_semaphore()
@@ -96,6 +101,8 @@
     for k in others:
         pl.semaphore_signal(barrier, inc=1, device_id=across(k), device_id_type=MESH)
 
+    for copy in small:
+        copy.wait()
     taps = [cw[n // 3, n % 3].astype(F32) for n in range(9)]
     wfwd[...] = jnp.concatenate(taps, axis=1).astype(BF16)
     flipped = jnp.concatenate([taps[8 - n] for n in range(9)], axis=0)
@@ -267,6 +274,9 @@
     gain1, bias1 = vec[0:1, :], vec[1:2, :]
     co1[0] = columns_of(0.5 * gain1 * scale1, C)
     co1[1] = columns_of(0.5 * (bias1 - mean1 * gain1 * scale1), C)
+    middle = jnp.floor(bias1 * (8.0 + 8.0 * jnp.tanh(0.5 * bias1)) + 0.5) * (1.0 / 16.0)
+    co1[2] = columns_of(middle, C)
+    gram[...] = jnp.zeros_like(gram)
 
     def activate(p, carry):
         h = p * R
@@ -279,16 +289,37 @@
             hid[h + j] = half
             slope[h + j] = 0.5 * u * (1.0 + half * (1.0 - t))
             ybuf[h + j] = y
-            rows.append(y)
-        block = dot(wproj[...], jnp.concatenate(rows, axis=1))
+            rows.append((y.astype(F32) - co1[2]).astype(BF16))
+        off = jnp.concatenate(rows, axis=1)
+        gram[...] += dot_nt(jnp.concatenate([off, jnp.ones((16, R * W), BF16)], axis=0), off)
+        return carry
+
+    lax.fori_loop(0, TH // R, activate, 0)
+    gram[C : C + 8, :] = gram[C : C + 8, :] * (1.0 / n_local)
+    gram[C + 8 : C + 16, :] = jnp.broadcast_to(middle[:, 0:C], (8, C))
+    table = gram[...]
+    high = table.astype(BF16)
+    rest = table - high.astype(F32)
+    mid = rest.astype(BF16)
+    low = (rest - mid.astype(F32)).astype(BF16)
+    turned = dot(jnp.concatenate([high, mid, low], axis=0), pw[...])
+    turned = turned[0 : C + 16] + turned[C + 16 : 2 * C + 32] + turned[2 * C + 32 :]
+    local = turned[C : C + 1]
+    spread_of = jnp.sum(turned[0:C] * pw[...].astype(F32), axis=0, keepdims=True) - n_local * local * local
+    local = local + turned[C + 8 : C + 9]
+    for k in range(nb3):
+        m3s[k : k + 1, :] = local[:, k * LANES : (k + 1) * LANES]
+        m3s[nb3 + k : nb3 + k + 1, :] = spread_of[:, k * LANES : (k + 1) * LANES]
+    exchange(m3s, m3r, 7)
+
+    def project(p, carry):
+        h = p * R
+        block = dot(wproj[...], jnp.concatenate([ybuf[h + j] for j in range(R)], axis=1))
         for j in range(R):
             wide[h + j] = block[:, j * W : (j + 1) * W]
         return carry
 
-    lax.fori_loop(0, TH // R, activate, 0)
-
-    moments(wide, CO, m3s)
-    exchange(m3s, m3r, 7)
+    lax.fori_loop(0, TH // R, project, 0)
 
     lt_c = dw.shape[1] // LANES
     lt_p = CO // LANES
@@ -342,8 +373,8 @@
 
         def slopes(p, carry):
             total, cross = carry
-            for j in range(4):
-                h = p * 4 + j
+            for j in range(8):
+                h = p * 8 + j
                 half = wide[h, c : c + step_c, :] * alpha + beta
                 t = jnp.tanh(half)
                 g = egrad[h, c : c + step_c, :]
@@ -355,7 +386,7 @@
             return total, cross
 
         zero = jnp.zeros((step_c, W), F32)
-        total, cross = lax.fori_loop(0, TH // 4, slopes, (zero, zero))
+        total, cross = lax.fori_loop(0, TH // 8, slopes, (zero, zero))
         firsts.append(jnp.sum(total, axis=1, keepdims=True))
         seconds.append(jnp.sum(cross, axis=1, keepdims=True))
     put_rows(q3s, jnp.concatenate(firsts, axis=0), jnp.concatenate(seconds, axis=0))
@@ -368,28 +399,33 @@
     vs[...] = jnp.zeros_like(vs)
     vs[0:nb3, :] = s3
     vs[nb3 : 2 * nb3, :] = q3
-    co3[0] = columns_of(0.5 * gain3 * scale3, CO)
     co3[1] = columns_of((-2.0 / M) * scale3 * q3, CO)
     co3[2] = columns_of((1.0 / M) * scale3 * (q3 * bias3 - gain3 * s3), CO)
 
     pg[...] = jnp.zeros_like(pg)
     dw[...] = jnp.zeros_like(dw)
+    ebuf[...] = jnp.zeros_like(ebuf)
+
+    def max_of(p):
+        return jnp.where(p < 0, 0, p)
 
     def unproject(p, carry):
         total, cross = carry
         h = p * R
-        rows = []
-        for j in range(R):
-            pieces = []
-            for c in range(0, CO, 64):
-                part = slice(c, c + 64)
-                grad = egrad[h + j, part, :] * co3[0, part, :] + wide[h + j, part, :] * co3[1, part, :]
-                pieces.append((grad + co3[2, part, :]).astype(BF16))
-            rows.append(jnp.concatenate(pieces, axis=0))
-        grads = jnp.concatenate(rows, axis=1)
+        pieces = []
+        for c in range(0, CO, 32):
+            part = slice(c, c + 32)
+            alpha, beta, gamma = co3[0, part, :], co3[1, part, :], co3[2, part, :]
+            rows = [
+                (egrad[h + j, part, :] * alpha + wide[h + j, part, :] * beta + gamma).astype(BF16) for j in range(R)
+            ]
+            pieces.append(jnp.concatenate(rows, axis=1))
+        grads = jnp.concatenate(pieces, axis=0)
         hidden = jnp.concatenate([ybuf[h + j] for j in range(R)], axis=1)
         pg[...] += dot_nt(hidden, grads)
         block = dot(pw[...], grads)
+        held = max_of(p - 1) * R
+        dw[:, 0 : 9 * C] += dot_nt(ebuf[...], stack(xs, held))
         rows = []
         for j in range(R):
             e = block[:, j * W : (j + 1) * W] * slope[h + j]
@@ -397,20 +433,22 @@
             rows.append(e.astype(BF16))
             total = total + e
             cross = cross + e * hid[h + j]
-        dw[:, 0 : 9 * C] += dot_nt(jnp.concatenate(rows, axis=1), stack(xs, h))
+        ebuf[...] = jnp.concatenate(rows, axis=1)
         return total, cross
 
     zero = jnp.zeros((C, W), F32)
     total, cross = lax.fori_loop(0, TH // R, unproject, (zero, zero))
+    dw[:, 0 : 9 * C] += dot_nt(ebuf[...], stack(xs, TH - R))
+
     for r in range(C // 16):
         rows = slice(r * 16, (r + 1) * 16)
         for t in range(lt_c):
             tiles[r * lt_c + t] = dw[rows, t * LANES : (t + 1) * LANES]
         for t in range(lt_p):
             tiles[n_conv + r * lt_p + t] = pg[rows, t * LANES : (t + 1) * LANES]
+    scatter(tiles, rtiles, 0, n_tiles, 10)
     put_rows(q1s, jnp.sum(total, axis=1, keepdims=True), jnp.sum(cross, axis=1, keepdims=True))
     exchange(q1s, q1r, 9)
-    scatter(tiles, rtiles, 0, n_tiles, 10)
 
     arrived(q1r, 9)
     s1 = jnp.sum(q1r[:, 0:nb1, :], axis=0)
@@ -534,9 +572,20 @@
     put.wait()
 
 
-def finish(img, agr, sums, o_img, o_cw, o_pw, o_g1, o_b1, o_g3, o_b3, sem):
-    copy = pltpu.make_async_copy(img, o_img, sem)
-    copy.start()
+def finish(img, agr_in, sums_in, o_img, o_cw, o_pw, o_g1, o_b1, o_g3, o_b3, held, agr, sums, sem):
+    small = [pltpu.make_async_copy(agr_in, agr, sem.at[0]), pltpu.make_async_copy(sums_in, sums, sem.at[1])]
+    parts = 4
+    step = held.shape[0] // parts
+    cuts = [pl.ds(k * step, step) for k in range(parts)]
+    come = [pltpu.make_async_copy(img.at[0, 0, c], held.at[c], sem.at[2 + k]) for k, c in enumerate(cuts)]
+    leave = [pltpu.make_async_copy(held.at[c], o_img.at[0, 0, c], sem.at[2 + parts + k]) for k, c in enumerate(cuts)]
+    for copy in small + come:
+        copy.start()
+    for there, back in zip(come, leave):
+        there.wait()
+        back.start()
+    for copy in small:
+        copy.wait()
     C = o_pw.shape[0]
     nb3 = o_g3.shape[0]
     lt_p = o_pw.shape[1] // LANES
@@ -554,7 +603,8 @@
         line = jnp.concatenate(line, axis=1)
         for n in range(9):
             o_cw[n // 3, n % 3, rows, :] = line[:, n * C : (n + 1) * C]
-    copy.wait()
+    for copy in leave:
+        copy.wait()
 
 
 def solution(mesh):
@@ -583,21 +633,22 @@
             vm((16, LANES), BF16), vm((n_dp, 16, LANES), BF16), vm((8, LANES), F32), vm((n_dp, 8, LANES), F32),
             vm((16, LANES), BF16), vm((NG, 16, LANES), BF16), vm((8, LANES), F32),
             vm((3, CO, W), F32), vm((3, C, W), F32),
-            vm((C + 16, wide_c), F32), vm((n_conv, 24, LANES), F32), vm((NG, 24, LANES), F32),
-            pltpu.SemaphoreType.DMA((15,)), pltpu.SemaphoreType.DMA((15,)), pltpu.SemaphoreType.DMA((3,)),
+            vm((C + 16, wide_c), F32), vm((n_conv, 24, LANES), F32), vm((NG, 24, LANES), F32), vm((C + 16, C), F32), vm((C, 4 * W), BF16),
+            vm((3, 3, C, C), BF16), vm((C, CO), BF16), vm((1, C), F32), vm((1, C), F32), vm((nb3, LANES), F32),
+            vm((nb3, LANES), F32),
+            pltpu.SemaphoreType.DMA((15,)), pltpu.SemaphoreType.DMA((15,)), pltpu.SemaphoreType.DMA((9,)),
         ]
         vspec = pl.BlockSpec(memory_space=pltpu.VMEM)
         aspec = pl.BlockSpec(memory_space=pl.ANY)
-        hspec = pl.BlockSpec(memory_space=pltpu.HBM)
         shape = jax.ShapeDtypeStruct
         img, tiles, sums = pl.pallas_call(
             functools.partial(kernel, n_sp, n_bn, n_dp, 1.0 / float(n_sp * TH * W)),
             out_shape=(shape(images.shape, BF16), shape((n_tiles, 16, LANES), BF16), shape((8, LANES), F32)),
-            in_specs=[hspec, hspec] + [vspec] * 6,
+            in_specs=[aspec] * 8,
             out_specs=(aspec, vspec, vspec),
             scratch_shapes=scratch,
             compiler_params=pltpu.CompilerParams(
-                collective_id=0, has_side_effects=True, vmem_limit_bytes=55200000
+                collective_id=0, has_side_effects=True, vmem_limit_bytes=65000000
             ),
         )(
             images, out_grad, conv_weight, proj_weight, gain_one.reshape(1, C), shift_one.reshape(1, C),
@@ -609,10 +660,12 @@
                 shape(images.shape, BF16), shape((3, 3, C, C), F32), shape((C, CO), F32), shape((1, C), F32),
                 shape((1, C), F32), shape((nb3, LANES), F32), shape((nb3, LANES), F32),
             ),
-            in_specs=[aspec, vspec, vspec],
+            in_specs=[aspec] * 3,
             out_specs=(aspec,) + (vspec,) * 6,
-            scratch_shapes=[pltpu.SemaphoreType.DMA],
-            compiler_params=pltpu.CompilerParams(vmem_limit_bytes=4 * 1024 * 1024),
+            scratch_shapes=[
+                vm((C, TH, W), BF16), vm((n_tiles, 16, LANES), BF16), vm((8, LANES), F32), pltpu.SemaphoreType.DMA((10,))
+            ],
+            compiler_params=pltpu.CompilerParams(vmem_limit_bytes=65000000),
         )(img, tiles, sums)
         return (
             got[0], got[1], got[2], got[3].reshape(C), got[4].reshape(C), got[5].reshape(CO), got[6].reshape(CO),

time: 79.6 us -> 77.7 us (0.976)
  local copies, waits for them, and re-layouts: 4.33 us -> 0 us
  Pallas kernels: 73.8 us -> 76.9 us
    unnamed x12 -> x0, local copies, waits for them, and re-layouts: 4.33 us -> none
    pallas_call x1, Pallas kernels: 72.2 us -> 74.2 us  [step(): pl.pallas_call(functools.partial(kernel, n_sp, n_bn, n_dp, 1.0 / float(n_...]
    pallas_call x1, Pallas kernels: 1.6 us -> 2.72 us  [step(): pl.pallas_call(finish, out_shape=(shape(images.shape, BF16), shape((3, 3,...]
where the time goes in v3:
time: 77.7 us; the launch traced here: 77.5 us
  Pallas kernels  76.9 us (99%)
    pallas_call x1, Pallas kernels, step(): pl.pallas_call(functools.partial(kernel, n_sp, n_bn, n_dp, 1.0 / float(n_...  74.2 us
    pallas_call x1, Pallas kernels, step(): pl.pallas_call(finish, out_shape=(shape(images.shape, BF16), shape((3, 3,...  2.72 us

profile of v3, /device:TPU:6, one launch (start us, length us, event | category | flops | bytes accessed | tf_op | source)
XLA Modules:
  0.0 77.5 jit_solution(10001602382135500363)
XLA Ops:
  0.6 74.2 %shard_map.135 = (bf16[1,1,64,40,128]{4,3,2,1,0:T(8,128)(2,1)}, bf16[28,16,128]{2,1,0:T(8,128)(2,1)}, f32[8,128]{1,0:T(8,128)}) custom-call(bf16[1,1,64,40,128]{4,3,2,1,0:T(8,128)(2,1)} %img.1, bf16[1,1,256,40,128]{4,3,2,1,0:T(8,128)(2,1)} %cot.1, bf16[3,3,64,64]{3,2,1,0:T(8,128)(2,1)} %cw_in.1, bf16[64,256]{1,0:T(8,128)(2,1)} %pw_in.1, f32[1,64]{1,0:T(1,128)} %bitcast.10, ...), custom_call_target="tpu_custom_call" | custom-call | tf_op jit(solution)/shard_map/pallas_call | solution.py:644
  74.8 2.7 %shard_map.136 = (bf16[1,1,64,40,128]{4,3,2,1,0:T(8,128)(2,1)}, f32[3,3,64,64]{3,2,1,0:T(8,128)}, f32[64,256]{1,0:T(8,128)}, f32[1,64]{1,0:T(1,128)}, f32[1,64]{...) custom-call(bf16[1,1,64,40,128]{4,3,2,1,0:T(8,128)(2,1)} %get-tuple-element.17.img, ...), custom_call_target="tpu_custom_call" | custom-call | tf_op jit(solution)/shard_map/pallas_call | solution.py:657

commit v4 on v3

--- a/solution.py
+++ b/solution.py
@@ -446,9 +446,9 @@
             tiles[r * lt_c + t] = dw[rows, t * LANES : (t + 1) * LANES]
         for t in range(lt_p):
             tiles[n_conv + r * lt_p + t] = pg[rows, t * LANES : (t + 1) * LANES]
-    scatter(tiles, rtiles, 0, n_tiles, 10)
     put_rows(q1s, jnp.sum(total, axis=1, keepdims=True), jnp.sum(cross, axis=1, keepdims=True))
     exchange(q1s, q1r, 9)
+    scatter(tiles, rtiles, 0, n_tiles, 10)
 
     arrived(q1r, 9)
     s1 = jnp.sum(q1r[:, 0:nb1, :], axis=0)

time: 77.7 us -> 74.6 us (0.960)
  Pallas kernels: 76.9 us -> 73.7 us
    pallas_call x1, Pallas kernels: 74.2 us -> 71 us  [step(): pl.pallas_call(functools.partial(kernel, n_sp, n_bn, n_dp, 1.0 / float(n_...]
where the time goes in v4:
time: 74.6 us; the launch traced here: 74.3 us
  Pallas kernels  73.7 us (99%)
    pallas_call x1, Pallas kernels, step(): pl.pallas_call(functools.partial(kernel, n_sp, n_bn, n_dp, 1.0 / float(n_...  71 us
    pallas_call x1, Pallas kernels, step(): pl.pallas_call(finish, out_shape=(shape(images.shape, BF16), shape((3, 3,...  2.72 us

profile of v4, /device:TPU:6, one launch (start us, length us, event | category | flops | bytes accessed | tf_op | source)
XLA Modules:
  0.0 74.3 jit_solution(16846633756196575223)
XLA Ops:
  0.6 71.0 %shard_map.135 = (bf16[1,1,64,40,128]{4,3,2,1,0:T(8,128)(2,1)}, bf16[28,16,128]{2,1,0:T(8,128)(2,1)}, f32[8,128]{1,0:T(8,128)}) custom-call(bf16[1,1,64,40,128]{4,3,2,1,0:T(8,128)(2,1)} %img.1, bf16[1,1,256,40,128]{4,3,2,1,0:T(8,128)(2,1)} %cot.1, bf16[3,3,64,64]{3,2,1,0:T(8,128)(2,1)} %cw_in.1, bf16[64,256]{1,0:T(8,128)(2,1)} %pw_in.1, f32[1,64]{1,0:T(1,128)} %bitcast.10, ...), custom_call_target="tpu_custom_call" | custom-call | tf_op jit(solution)/shard_map/pallas_call | solution.py:644
  71.6 2.7 %shard_map.136 = (bf16[1,1,64,40,128]{4,3,2,1,0:T(8,128)(2,1)}, f32[3,3,64,64]{3,2,1,0:T(8,128)}, f32[64,256]{1,0:T(8,128)}, f32[1,64]{1,0:T(1,128)}, f32[1,64]{...) custom-call(bf16[1,1,64,40,128]{4,3,2,1,0:T(8,128)(2,1)} %get-tuple-element.17.img, ...), custom_call_target="tpu_custom_call" | custom-call | tf_op jit(solution)/shard_map/pallas_call | solution.py:657
